TPU v7x, 32 devices: a whole 2x2x4 slice. The times are simulated.
32 devices in a mesh: crops: 2 (over y), rows: 4 (over z), chan: 2 (over x), sub: 2 (over core).
Axes of the slice: x: 2, y: 2, z: 4, core: 2. Of those that a mesh axis runs over, the one named last changes fastest.
Arguments:
- pair: bfloat16 [64, 32, 128], P(('crops', 'rows', 'sub')), parts along dimension 0, may hold values from -6 to 6
- residue_mask: int32 [64], P('crops'), parts along dimension 0, may hold values from 0 to 1, as said below
- in_gain: float32 [2, 128], replicated, may hold values from 0.1 to 1.9
- in_bias: float32 [2, 128], replicated, may hold values from -3 to 3
- projections: bfloat16 [2, 4, 128, 128], P(None, None, None, 'chan'), may hold values from -0.5 to 0.5
- gate_weight: bfloat16 [2, 128, 128], replicated, may hold values from -0.5 to 0.5
- out_gain: float32 [2, 128], replicated, may hold values from 0.1 to 1.9
- out_bias: float32 [2, 128], replicated, may hold values from -3 to 3
- out_weight: bfloat16 [2, 128, 128], replicated, may hold values from -0.5 to 0.5
Outputs:
- pair_out: bfloat16 [64, 32, 128], P(('crops', 'rows', 'sub'), 'chan'), parts along dimension 0
There are 2 independent parts, one for each index of `crops`. A program takes and returns all parts, laid end to end along the dimension named above; an argument that names none is the same for every part. Nothing has to cross between parts.
Inputs may be any that keep to these rules, and one draw needn't show every extreme that they name: `residue_mask`: residue 0 is always present and residue 32 - 1 is always a gap or padding.
All inputs are finite; a program needn't handle non-finite values.
Results may differ from a plain program's by a relative error of at most 0.012.
Values may be sent and summed in bfloat16 or wider, within the bound.
No kernel may reach another device: no remote copies, remote signals or barrier semaphores. Data moves between devices by JAX's collectives and lax.ppermute only.
A program may use at most 64 MiB of HBM per device.

v0:
```python
import jax
import jax.numpy as jnp
from jax import lax
from jax.sharding import PartitionSpec as P

epsilon = 1e-05


def normalize(values, reduce_axis):
    centre = jnp.mean(values, axis=reduce_axis, keepdims=True)
    centred = values - centre
    spread = jnp.mean(centred * centred, axis=reduce_axis, keepdims=True)
    return centred * lax.rsqrt(spread + epsilon)


def shards(
    pair, residue_mask, in_gain, in_bias, projections, gate_weight, out_gain, out_bias, out_weight
):
    rows_block = pair.shape[0]
    length = pair.shape[1]
    chan_count = lax.axis_size("chan")
    chan_index = lax.axis_index("chan")
    quarter = length // chan_count
    row_start = lax.axis_index(("rows", "sub")) * rows_block
    mask_float = residue_mask.astype(jnp.float32)
    own_mask = lax.dynamic_slice_in_dim(mask_float, row_start, rows_block)
    pair_mask = own_mask[None, :, None] * mask_float[None, None, :]

    def project(full_rows, layer_index):
        normed = (
            normalize(full_rows.astype(jnp.float32), 2) * in_gain[layer_index]
            + in_bias[layer_index]
        ).astype(jnp.bfloat16)
        projected = jnp.einsum(
            "ikc,qch->qhik", normed, projections[layer_index], preferred_element_type=jnp.float32
        )
        left_edges = (jax.nn.sigmoid(projected[0]) * projected[1] * pair_mask).astype(jnp.bfloat16)
        right_edges = (jax.nn.sigmoid(projected[2]) * projected[3] * pair_mask).astype(jnp.bfloat16)
        return (normed, left_edges, right_edges)

    def finish(triangle, normed, residual, layer_index):
        gathered = lax.all_to_all(triangle, "chan", split_axis=2, concat_axis=0, tiled=True)
        whole_float = gathered.astype(jnp.float32)
        scaled = (
            normalize(whole_float, 0) * out_gain[layer_index][:, None, None]
            + out_bias[layer_index][:, None, None]
        ).astype(jnp.bfloat16)
        update = jnp.einsum(
            "hij,hc->ijc", scaled, out_weight[layer_index], preferred_element_type=jnp.float32
        )
        normed_part = lax.dynamic_slice_in_dim(normed, chan_index * quarter, quarter, 1)
        gating = jax.nn.sigmoid(
            jnp.einsum(
                "ijc,cd->ijd",
                normed_part,
                gate_weight[layer_index],
                preferred_element_type=jnp.float32,
            )
        )
        return (residual.astype(jnp.float32) + gating * update).astype(jnp.bfloat16)

    normed, left_edges, right_edges = project(pair, 0)
    triangle = jnp.einsum(
        "hik,hjk->hij",
        left_edges,
        lax.all_gather(right_edges, ("rows", "sub"), axis=1, tiled=True),
        preferred_element_type=jnp.float32,
    ).astype(jnp.bfloat16)
    own_quarter = lax.dynamic_slice_in_dim(pair, chan_index * quarter, quarter, 1)
    layer_one = finish(triangle, normed, own_quarter, 0)
    full_rows = lax.all_gather(layer_one, "chan", axis=1, tiled=True)
    normed, left_edges, right_edges = project(full_rows, 1)
    left_cols, right_cols = (
        lax.all_to_all(left_edges, ("rows", "sub"), split_axis=2, concat_axis=1, tiled=True),
        lax.all_to_all(right_edges, ("rows", "sub"), split_axis=2, concat_axis=1, tiled=True),
    )
    triangle = jnp.einsum(
        "hki,hkj->hij",
        left_cols,
        lax.all_gather(right_cols, ("rows", "sub"), axis=2, tiled=True),
        preferred_element_type=jnp.float32,
    )
    return finish(triangle.astype(jnp.bfloat16), normed, layer_one, 1)


def solution(mesh):
    placed = (
        P(("crops", "rows", "sub"), None, None),
        P("crops"),
        P(),
        P(),
        P(None, None, None, "chan"),
        P(),
        P(),
        P(),
        P(),
    )
    return jax.shard_map(
        shards,
        mesh=mesh,
        in_specs=placed,
        out_specs=P(("crops", "rows", "sub"), "chan", None),
        check_vma=False,
    )
```

profile of v0, /device:TPU:0, one launch (start us, length us, event | category | flops | bytes accessed | tf_op | source)
XLA Modules:
  0.0 73.9 jit_solution(12154159398881067945)
XLA Ops:
  0.0 0.6 copy-done.8
  0.8 0.8 %convert_reduce_fusion.1 = f32[4,32]{1,0:T(4,128)S(1)} fusion(bf16[4,32,128]{2,1,0:T(8,128)(2,1)} %param.9), kind=kLoop, calls=%fused_computation.21 | loop fusion | flops 32640 | bytes 33280 | tf_op jit(solution)/shard_map/reduce_sum | solution.py:10
  1.7 0.2 fusion.18
  1.9 0.1 fusion.21
  2.0 0.2 convolution_bitcast_fusion.1
  2.3 15.9 %all_gather.9 = bf16[64,32,32]{0,2,1:T(8,128)(2,1)S(1)} all-gather(bf16[64,4,32]{0,2,1:T(8,128)(2,1)S(1)} %get-tuple-element.11), channel_id=1, replica_groups=mesh['crops'=2,'rows'=4,'chan'=2,'sub'=2] {'rows','sub'}, dimensions={1}, use_global_device_ids=true | all-gather | bytes 147456 | tf_op jit(solution)/shard_map/all_gather | solution.py:66
  18.2 0.8 %copy.58 = bf16[64,32,32]{2,1,0:T(8,128)(2,1)S(1)} copy(bf16[64,32,32]{0,2,1:T(8,128)(2,1)S(1)} %all_gather.9) | data formatting | bytes 262144 | tf_op jit(solution)/shard_map/all_gather | solution.py:66
  19.0 0.1 copy.57
  19.1 0.4 convolution_convert_fusion.1
  19.5 0.1 copy.59
  19.6 0.7 reshape.162
  20.3 3.2 %all-to-all-start = ((bf16[2,2,2048]{2,1,0:T(2,128)(2,1)}), bf16[2,2,2048]{2,1,0:T(2,128)(2,1)S(1)}, u32[]{:S(2)}, u32[]{:S(2)}) async-start(bf16[2,2,2048]{2,1,0:T(2,128)(2,1)} %reshape.162), calls=%async_computation | async-start | bytes 32768 | tf_op jit(solution)/shard_map/all_to_all | solution.py:42
  23.6 0.1 fusion.7
  23.8 0.5 copy-done.5
  24.5 2.9 %all-to-all-done = bf16[2,2,2048]{2,1,0:T(2,128)(2,1)S(1)} async-done(((bf16[2,2,2048]{2,1,0:T(2,128)(2,1)}), bf16[2,2,2048]{2,1,0:T(2,128)(2,1)S(1)}, u32[]{:S(2)}, u32[]{:S(2)}) %all-to-all-start) | async-done | bytes 16416 | tf_op jit(solution)/shard_map/all_to_all | solution.py:42
  27.4 0.1 reshape.163
  27.5 0.1 fusion.60
  27.6 0.2 fusion.63
  27.8 0.1 fusion.66
  28.0 0.1 convert_element_type.92
  28.1 0.7 copy-done.2
  28.8 0.1 fusion.8
  28.9 4.4 %all_gather.10 = bf16[4,32,128]{2,1,0:T(8,128)(2,1)S(1)} all-gather(bf16[4,16,128]{2,1,0:T(8,128)(2,1)S(1)} %fusion.8), channel_id=1, replica_groups=mesh['crops'=2,'rows'=4,'chan'=2,'sub'=2] {'chan'}, dimensions={1}, use_global_device_ids=true | all-gather | bytes 49152 | tf_op jit(solution)/shard_map/all_gather | solution.py:71
  33.4 0.2 fusion.14
  33.6 0.1 fusion.17
  33.7 0.2 convolution_bitcast_fusion
  34.0 0.7 reshape.166
  34.7 4.7 %all-to-all-start.2 = ((bf16[8,2,512]{2,1,0:T(2,128)(2,1)}), bf16[8,2,512]{2,1,0:T(2,128)(2,1)S(1)}, u32[]{:S(2)}, u32[]{:S(2)}) async-start(bf16[8,2,512]{2,1,0:T(2,128)(2,1)} %reshape.166), calls=%async_computation.2 | async-start | bytes 32768 | tf_op jit(solution)/shard_map/all_to_all | solution.py:75
  39.6 0.7 reshape.164
  40.3 4.8 %all-to-all-done.2 = bf16[8,2,512]{2,1,0:T(2,128)(2,1)S(1)} async-done(((bf16[8,2,512]{2,1,0:T(2,128)(2,1)}), bf16[8,2,512]{2,1,0:T(2,128)(2,1)S(1)}, u32[]{:S(2)}, u32[]{:S(2)}) %all-to-all-start.2) | async-done | bytes 16416 | tf_op jit(solution)/shard_map/all_to_all | solution.py:75
  45.1 3.3 %all-to-all-start.1 = ((bf16[8,2,512]{2,1,0:T(2,128)(2,1)}), bf16[8,2,512]{2,1,0:T(2,128)(2,1)S(1)}, u32[]{:S(2)}, u32[]{:S(2)}) async-start(bf16[8,2,512]{2,1,0:T(2,128)(2,1)} %reshape.164), calls=%async_computation.1 | async-start | bytes 32768 | tf_op jit(solution)/shard_map/all_to_all | solution.py:74
  48.4 0.1 reshape.167
  48.5 14.7 %all_gather.11 = bf16[64,32,32]{0,1,2:T(8,128)(2,1)S(1)} all-gather(bf16[64,32,4]{0,1,2:T(8,128)(2,1)S(1)} %bitcast.191), channel_id=1, replica_groups=mesh['crops'=2,'rows'=4,'chan'=2,'sub'=2] {'rows','sub'}, dimensions={2}, use_global_device_ids=true | all-gather | bytes 147456 | tf_op jit(solution)/shard_map/all_gather | solution.py:80
  63.2 0.8 %copy.68 = bf16[64,32,32]{1,2,0:T(8,128)(2,1)S(1)} copy(bf16[64,32,32]{0,1,2:T(8,128)(2,1)S(1)} %all_gather.11) | data formatting | bytes 262144 | tf_op jit(solution)/shard_map/all_gather | solution.py:80
  64.0 0.1 reshape.165
  64.1 0.1 copy.67
  64.2 0.4 convolution_convert_fusion
  64.6 0.1 copy.69
  64.7 0.7 reshape.168
  65.4 3.2 %all-to-all-start.3 = ((bf16[2,2,2048]{2,1,0:T(2,128)(2,1)}), bf16[2,2,2048]{2,1,0:T(2,128)(2,1)S(1)}, u32[]{:S(2)}, u32[]{:S(2)}) async-start(bf16[2,2,2048]{2,1,0:T(2,128)(2,1)} %reshape.168), calls=%async_computation.3 | async-start | bytes 32768 | tf_op jit(solution)/shard_map/all_to_all | solution.py:42
  68.7 0.1 fusion.3
  68.8 3.7 %all-to-all-done.3 = bf16[2,2,2048]{2,1,0:T(2,128)(2,1)S(1)} async-done(((bf16[2,2,2048]{2,1,0:T(2,128)(2,1)}), bf16[2,2,2048]{2,1,0:T(2,128)(2,1)S(1)}, u32[]{:S(2)}, u32[]{:S(2)}) %all-to-all-start.3) | async-done | bytes 16416 | tf_op jit(solution)/shard_map/all_to_all | solution.py:42
  72.5 0.1 reshape.169
  72.6 0.1 fusion.52
  72.7 0.2 fusion.55
  72.9 0.1 fusion.58
  73.1 0.1 convert_element_type.104
  73.1 0.7 %fusion.9 = bf16[4,16,128]{2,1,0:T(8,128)(2,1)} fusion(f32[4,16,128]{2,1,0:T(8,128)S(1)} %fusion.3, bf16[128,4,16]{0,2,1:T(8,128)(2,1)S(1)} %convert_element_type.104, bf16[2,128,128]{2,1,0:T(8,128)(2,1)S(1)} %copy-done.2, bf16[4,16,128]{2,1,0:T(8,128)(2,1)S(1)} %fusion.8), kind=kOutput, calls=%fused_computation.17 | convolution fusion | flops 2129920 | bytes 114688 | tf_op jit(solution)/shard_map/hij,hc->ijc/dot_general | solution.py:48
  (44 shorter events, 1.0 us)
Async XLA Ops:
  0.0 0.7 copy-start.8
  0.0 1.9 %copy-start.3 = (f32[2,128]{1,0:T(2,128)S(1)}, f32[2,128]{1,0:T(2,128)}, u32[]{:S(2)}) copy-start(f32[2,128]{1,0:T(2,128)} %param.12) | copy-start | bytes 3076
  0.0 1.9 %copy-start.4 = (f32[2,128]{1,0:T(2,128)S(1)}, f32[2,128]{1,0:T(2,128)}, u32[]{:S(2)}) copy-start(f32[2,128]{1,0:T(2,128)} %param.11) | copy-start | bytes 3076
  0.0 1.7 %copy-start = (bf16[4,32,128]{2,1,0:T(8,128)(2,1)S(1)}, bf16[4,32,128]{2,1,0:T(8,128)(2,1)}, u32[]{:S(2)}) copy-start(bf16[4,32,128]{2,1,0:T(8,128)(2,1)} %param.9) | copy-start | bytes 98308
  0.0 2.0 %copy-start.1 = (bf16[2,4,128,64]{2,3,1,0:T(8,128)(2,1)S(1)}, bf16[2,4,128,64]{2,3,1,0:T(8,128)(2,1)}, u32[]{:S(2)}) copy-start(bf16[2,4,128,64]{2,3,1,0:T(8,128)(2,1)} %param.13) | copy-start | bytes 393220
  19.6 4.0 %copy-start.7 = (bf16[2,128,128]{2,1,0:T(8,128)(2,1)S(1)}, bf16[2,128,128]{2,1,0:T(8,128)(2,1)}, u32[]{:S(2)}) copy-start(bf16[2,128,128]{2,1,0:T(8,128)(2,1)} %param.14) | copy-start | bytes 196612
  20.3 7.1 %all-to-all-start = ((bf16[2,2,2048]{2,1,0:T(2,128)(2,1)}), bf16[2,2,2048]{2,1,0:T(2,128)(2,1)S(1)}, u32[]{:S(2)}, u32[]{:S(2)}) async-start(bf16[2,2,2048]{2,1,0:T(2,128)(2,1)} %reshape.162), calls=%async_computation | async-start | bytes 32768 | tf_op jit(solution)/shard_map/all_to_all | solution.py:42
  23.6 0.7 copy-start.5
  23.6 0.7 copy-start.6
  27.9 0.8 %copy-start.2 = (bf16[2,128,128]{2,1,0:T(8,128)(2,1)S(1)}, bf16[2,128,128]{2,1,0:T(8,128)(2,1)}, u32[]{:S(2)}) copy-start(bf16[2,128,128]{2,1,0:T(8,128)(2,1)} %param.17) | copy-start | bytes 196612
  34.7 10.3 %all-to-all-start.2 = ((bf16[8,2,512]{2,1,0:T(2,128)(2,1)}), bf16[8,2,512]{2,1,0:T(2,128)(2,1)S(1)}, u32[]{:S(2)}, u32[]{:S(2)}) async-start(bf16[8,2,512]{2,1,0:T(2,128)(2,1)} %reshape.166), calls=%async_computation.2 | async-start | bytes 32768 | tf_op jit(solution)/shard_map/all_to_all | solution.py:75
  45.1 18.9 %all-to-all-start.1 = ((bf16[8,2,512]{2,1,0:T(2,128)(2,1)}), bf16[8,2,512]{2,1,0:T(2,128)(2,1)S(1)}, u32[]{:S(2)}, u32[]{:S(2)}) async-start(bf16[8,2,512]{2,1,0:T(2,128)(2,1)} %reshape.164), calls=%async_computation.1 | async-start | bytes 32768 | tf_op jit(solution)/shard_map/all_to_all | solution.py:74
  65.4 7.1 %all-to-all-start.3 = ((bf16[2,2,2048]{2,1,0:T(2,128)(2,1)}), bf16[2,2,2048]{2,1,0:T(2,128)(2,1)S(1)}, u32[]{:S(2)}, u32[]{:S(2)}) async-start(bf16[2,2,2048]{2,1,0:T(2,128)(2,1)} %reshape.168), calls=%async_computation.3 | async-start | bytes 32768 | tf_op jit(solution)/shard_map/all_to_all | solution.py:42
where the time goes:
time: 74.4 us; the launch traced here: 73.9 us
  blocking collectives  35 us (47%)
  starting transfers between devices  14.5 us (19%)
  waiting for transfers between devices  11.4 us (15%)
  local copies, waits for them, and re-layouts  7.84 us (11%)
  other arithmetic  2.48 us (3%)
  matrix products  2.32 us (3%)
    all_gather x1, blocking collectives, shards(): lax.all_gather(right_edges, ('rows', 'sub'), axis=1, tiled=True)  15.9 us
    all_gather x1, blocking collectives, shards(): lax.all_gather(right_cols, ('rows', 'sub'), axis=2, tiled=True)  14.7 us
    all_to_all x2, waiting for transfers between devices, finish(): lax.all_to_all(triangle, 'chan', split_axis=2, concat_axis=0, tiled=True)  6.63 us
    all_to_all x2, starting transfers between devices, finish(): lax.all_to_all(triangle, 'chan', split_axis=2, concat_axis=0, tiled=True)  6.47 us
    unnamed x26, local copies, waits for them, and re-layouts  5.09 us
    all_to_all x1, waiting for transfers between devices, shards(): lax.all_to_all(right_edges, ('rows', 'sub'), split_axis=2, concat_axis=1,...  4.77 us
    all_to_all x1, starting transfers between devices, shards(): lax.all_to_all(right_edges, ('rows', 'sub'), split_axis=2, concat_axis=1,...  4.68 us
    all_gather x1, blocking collectives, shards(): full_rows = lax.all_gather(layer_one, 'chan', axis=1, tiled=True)  4.4 us
  transfers between devices with their start and end apart: 4, of which 3 were waited for; matrix products, arithmetic and copies ran while one was open for 3% of the time, Pallas kernels for 0%

commit v1 on v0

--- a/solution.py
+++ b/solution.py
@@ -1,9 +1,17 @@
+import functools
+
 import jax
 import jax.numpy as jnp
 from jax import lax
+from jax.experimental import pallas as pl
+from jax.experimental.pallas import tpu as pltpu
 from jax.sharding import PartitionSpec as P
 
+
 epsilon = 1e-05
+
+
+GATHER_LIMIT = 1 << 20
 
 
 def normalize(values, reduce_axis):
@@ -83,7 +91,331 @@
     return finish(triangle.astype(jnp.bfloat16), normed, layer_one, 1)
 
 
+def swap(value, axis, step):
+    count = lax.axis_size(axis)
+    return lax.ppermute(value, axis, [(i, i ^ step) for i in range(count)])
+
+
+def mm(a, b):
+    return jnp.dot(a, b, preferred_element_type=jnp.float32)
+
+
+def mmt(a, b):
+    return lax.dot_general(a, b, (((1,), (1,)), ((), ())), preferred_element_type=jnp.float32)
+
+
+def constants(c):
+    average = jnp.full((c, c), 1.0 / c, jnp.float32)
+    diagonal = lax.broadcasted_iota(jnp.int32, (c, c), 0) == lax.broadcasted_iota(jnp.int32, (c, c), 1)
+    centring = jnp.where(diagonal, 1.0 - 1.0 / c, -1.0 / c)
+    return centring.astype(jnp.bfloat16), average.astype(jnp.bfloat16)
+
+
+def layer_norm(values, gain, bias, centring, average):
+    centred = mm(values, centring)
+    spread = mm((centred * centred).astype(jnp.bfloat16), average)
+    return (centred * lax.rsqrt(spread + epsilon) * gain + bias).astype(jnp.bfloat16)
+
+
+def gated(half_gate, half_value):
+    return half_value * jnp.tanh(half_gate) + half_value
+
+
+class Stage:
+    def __init__(self, counts, state, small):
+        self.left, self.right, self.turned, self.gate, self.z, self.tri, self.w, self.mask, self.gw, self.ow = state
+        self.ig, self.ib = small
+        self.rows_count, self.chan_count, self.sub_count, self.size = counts
+        self.row = lax.axis_index("rows")
+        self.chan = lax.axis_index("chan")
+        self.sub = lax.axis_index("sub")
+        self.length, _, self.c = self.z.shape
+        self.h = self.left.shape[2]
+        self.chip = self.size * self.sub_count
+        self.centring, self.average = constants(self.c)
+
+    def at(self, rs, ss):
+        return ((self.row ^ rs) * self.sub_count + (self.sub ^ ss)) * self.size
+
+    def tile(self, rs):
+        return pl.multiple_of((self.row ^ rs) * self.chip, self.chip)
+
+    def norm(self, x, layer):
+        return layer_norm(x, self.ig[layer:layer + 1], self.ib[layer:layer + 1], self.centring, self.average)
+
+    def edges(self, blocks):
+        area = self.size * self.length
+        x = jnp.concatenate([b.reshape(area, self.c) for _, b in blocks], 0)
+        normed = self.norm(x, 0)
+        places = [pl.ds(self.at(*where), self.size) for where, _ in blocks]
+        both = [self.mask[p][:, None, :] * self.mask[...][None] for p in places]
+        shape = (self.size, self.length, self.h)
+
+        def part(v, i):
+            return v[i * area:(i + 1) * area].reshape(shape)
+
+        for ref, q in ((self.left, 0), (self.right, 2)):
+            p = mmt(normed, self.w[0, q:q + 2].reshape(2 * self.h, self.c))
+            for i, place in enumerate(places):
+                ref[place] = gated(part(p[:, :self.h], i), part(p[:, self.h:], i) * both[i])
+        g = jnp.tanh(mm(normed, self.gw[0]))
+        for i, place in enumerate(places):
+            self.gate[place] = part(g, i)
+            self.z[place] = part(x.astype(jnp.float32), i)
+
+    def turn(self, rs):
+        tile = self.tile(rs)
+        self.turned[:, pl.ds(tile, self.chip), :] = jnp.swapaxes(self.right[pl.ds(tile, self.chip)], 0, 1)
+
+    def triangle(self, ks, chips):
+        tiles = [pl.ds(self.tile(rs), self.chip) for rs in chips]
+
+        def inner(m, acc):
+            rs = [self.turned[m, t, :] for t in tiles]
+            out = []
+            for i, k in enumerate(ks):
+                l = self.left[k, pl.ds(m, 1), :]
+                out += [acc[i * len(rs) + j] + l * r for j, r in enumerate(rs)]
+            return tuple(out)
+
+        zero = tuple(jnp.zeros((self.chip, self.h), jnp.float32) for _ in range(len(ks) * len(tiles)))
+        acc = lax.fori_loop(0, self.length, inner, zero, unroll=8)
+        for i, k in enumerate(ks):
+            for j, t in enumerate(tiles):
+                self.tri[k, t, :] = acc[i * len(tiles) + j]
+
+    def block_rows(self, *places):
+        return [self.at(*p) + i for p in places for i in range(self.size)]
+
+    def chip_rows(self, rs):
+        return [self.tile(rs) + i for i in range(self.chip)]
+
+
+def first_kernel(counts, where, *refs):
+    chan_count = counts[1]
+    n = len(where)
+    blocks, weights = refs[:n], refs[n:n + chan_count]
+    mask_ref, ig_ref, ib_ref, pair_hbm, gw_hbm, ow_hbm = refs[n + chan_count:n + chan_count + 6]
+    state = refs[n + chan_count + 6:n + chan_count + 16]
+    pair_ref, gw_raw, ow_raw, sems = refs[n + chan_count + 16:]
+    pairs = ((pair_hbm, pair_ref), (gw_hbm, gw_raw), (ow_hbm, ow_raw))
+    copies = [pltpu.make_async_copy(src, dst, sems.at[i]) for i, (src, dst) in enumerate(pairs)]
+    for copy in copies:
+        copy.start()
+    s = Stage(counts, state, (ig_ref, ib_ref))
+    part = s.h // chan_count
+    half = jnp.bfloat16(0.5)
+    for i in range(chan_count):
+        at = pl.multiple_of((s.chan ^ i) * part, part)
+        s.w[:, :, pl.ds(at, part), :] = weights[i][...] * half
+    across = mask_ref[...].astype(jnp.float32)
+    square = (s.length, s.length)
+    diagonal = lax.broadcasted_iota(jnp.int32, square, 0) == lax.broadcasted_iota(jnp.int32, square, 1)
+    s.mask[...] = mm(jnp.where(diagonal, across, 0.0).astype(jnp.bfloat16), jnp.ones((s.length, s.h), jnp.bfloat16))
+    copies[1].wait()
+    s.gw[...] = gw_raw[...] * half
+    copies[0].wait()
+    s.edges([((0, 0), pair_ref[...])] + [(w, b[...]) for w, b in zip(where, blocks)])
+    copies[2].wait()
+    s.ow[...] = ow_raw[...] * half
+    for rs in (0, 1):
+        s.turn(rs)
+    for rs in (0, 1):
+        s.triangle(s.chip_rows(rs), (0, 1))
+
+
+def next_kernel(counts, where, block_ref, ig_ref, ib_ref, *refs):
+    s = Stage(counts, refs[len(refs) // 2:], (ig_ref, ib_ref))
+    size = counts[3]
+    s.edges([(w, block_ref[i * size:(i + 1) * size]) for i, w in enumerate(where)])
+    s.triangle(s.block_rows(*where), (0, 1))
+
+
+def last_kernel(counts, where, block_ref, ig_ref, ib_ref, *refs):
+    state = refs[:10]
+    og_hbm, ob_hbm, out_ref, l1_ref, r1_ref, n1_ref, og_ref, ob_ref, sems = refs[10:]
+    copies = [pltpu.make_async_copy(og_hbm, og_ref, sems.at[0]), pltpu.make_async_copy(ob_hbm, ob_ref, sems.at[1])]
+    for copy in copies:
+        copy.start()
+    s = Stage(counts, state, (ig_ref, ib_ref))
+    size, length, c, h = s.size, s.length, s.c, s.h
+    quarter = length // s.chan_count
+    s.edges([(w, block_ref[i * size:(i + 1) * size]) for i, w in enumerate(where)])
+    s.triangle(s.block_rows(*where), (0, 1))
+    others = tuple(range(2, s.rows_count))
+    for rs in others:
+        s.turn(rs)
+    for rs in range(s.rows_count):
+        s.triangle(s.chip_rows(rs), others)
+
+    def finish(tri, half_gate, residual, layer):
+        scaled = layer_norm(
+            tri.astype(jnp.bfloat16), og_ref[layer:layer + 1], ob_ref[layer:layer + 1], s.centring, s.average
+        )
+        update = mm(scaled, s.ow[layer])
+        return residual + (update * half_gate + update)
+
+    for copy in copies:
+        copy.wait()
+    chunk = length // 2
+    for b in range(2):
+        rows = slice(b * chunk, (b + 1) * chunk)
+        flat = (chunk * length, c)
+        z = finish(s.tri[rows].reshape(flat), s.gate[rows].reshape(flat), s.z[rows].reshape(flat), 0)
+        s.z[rows] = z.astype(jnp.bfloat16).astype(jnp.float32).reshape(chunk, length, c)
+
+    own = s.at(0, 0)
+    i_tile = s.tile(0)
+    j_at = pl.multiple_of(s.chan * quarter, quarter)
+    mask = s.mask[...]
+    zi = s.z[:, pl.ds(i_tile, s.chip), :].reshape(length * s.chip, c).astype(jnp.bfloat16)
+    mi = mask[:, None, :] * s.mask[pl.ds(i_tile, s.chip)][None]
+    p = mmt(s.norm(zi, 1), s.w[1, 0:2].reshape(2 * h, c))
+    shape = (length, s.chip, h)
+    l1_ref[...] = gated(p[:, :h].reshape(shape), p[:, h:].reshape(shape) * mi)
+    zj = s.z[:, pl.ds(j_at, quarter), :].reshape(length * quarter, c).astype(jnp.bfloat16)
+    nj = s.norm(zj, 1)
+    mj = mask[:, None, :] * s.mask[pl.ds(j_at, quarter)][None]
+    p = mmt(nj, s.w[1, 2:4].reshape(2 * h, c))
+    shape = (length, quarter, h)
+    r1_ref[...] = gated(p[:, :h].reshape(shape), p[:, h:].reshape(shape) * mj)
+    n1_ref[...] = nj.reshape(shape)
+
+    first = own - i_tile
+
+    def inner(k, acc):
+        r = r1_ref[k]
+        return tuple(a + l1_ref[k, pl.ds(first + i, 1), :] * r for i, a in enumerate(acc))
+
+    zero = tuple(jnp.zeros((quarter, h), jnp.float32) for _ in range(size))
+    tri = jnp.concatenate(lax.fori_loop(0, length, inner, zero, unroll=8), 0)
+    mine = pl.ds(own, size)
+    flat = (size * quarter, c)
+    gate = jnp.tanh(mm(n1_ref[mine].reshape(flat), s.gw[1]))
+    z = finish(tri, gate, s.z[mine, pl.ds(j_at, quarter), :].reshape(flat), 1)
+    out_ref[...] = z.astype(jnp.bfloat16).reshape(size, quarter, c)
+
+
+def in_vmem(value):
+    return pltpu.with_memory_space_constraint(value, pltpu.VMEM)
+
+
+def in_hbm(value):
+    return pltpu.with_memory_space_constraint(value, pltpu.HBM)
+
+
+VMEM = pl.BlockSpec(memory_space=pltpu.VMEM)
+HBM = pl.BlockSpec(memory_space=pltpu.HBM)
+
+
+def join_kernel(a_ref, b_ref, out_ref):
+    size = a_ref.shape[0]
+    out_ref[0:size] = a_ref[...]
+    out_ref[size:] = b_ref[...]
+
+
+def join(a, b):
+    return pl.pallas_call(
+        join_kernel,
+        out_shape=pltpu.VMEM((2 * a.shape[0], *a.shape[1:]), a.dtype),
+        in_specs=[VMEM, VMEM],
+        out_specs=VMEM,
+        compiler_params=pltpu.CompilerParams(vmem_limit_bytes=1 << 20),
+    )(in_vmem(a), in_vmem(b))
+
+
+def gathered(
+    pair, residue_mask, in_gain, in_bias, projections, gate_weight, out_gain, out_bias, out_weight
+):
+    rows_count, chan_count, sub_count = (lax.axis_size(a) for a in ("rows", "chan", "sub"))
+    size, length, c = pair.shape
+    h = out_weight.shape[1]
+    counts = (rows_count, chan_count, sub_count, size)
+    turned = jnp.swapaxes(projections, 2, 3)
+    cross = [
+        (r * sub_count + s, (r ^ 1) * sub_count + (s ^ 1)) for r in range(rows_count) for s in range(sub_count)
+    ]
+    first = lax.ppermute(pair, ("rows", "sub"), cross)
+    beside = swap(pair, "sub", 1)
+    weights = [turned] + [swap(turned, "chan", i) for i in range(1, chan_count)]
+    joined = join(beside, first)
+    away = swap(joined, "rows", 2)
+    back = swap(first, "sub", 1)
+    last = swap(away, "sub", 1)
+
+    wide = (length, length, c)
+    state = [
+        jax.ShapeDtypeStruct(shape, dtype)
+        for shape, dtype in (
+            *[(wide, jnp.float32)] * 6,
+            ((2, 4, h, c), jnp.bfloat16),
+            ((length, h), jnp.float32),
+            ((2, c, c), jnp.bfloat16),
+            ((2, h, c), jnp.bfloat16),
+        )
+    ]
+    held = [pltpu.VMEM(t.shape, t.dtype) for t in state]
+    small = [in_gain, in_bias]
+
+    def params(mib):
+        return pltpu.CompilerParams(vmem_limit_bytes=mib << 20)
+
+    def cost(rows):
+        return pl.CostEstimate(flops=rows * 128 * 128 * 16, bytes_accessed=0, transcendentals=0)
+
+    near = [beside, first, back, *weights, residue_mask[None], *small]
+    far = [pair, gate_weight, out_weight]
+    state = pl.pallas_call(
+        functools.partial(first_kernel, counts, ((0, 1), (1, 1), (1, 0))),
+        out_shape=held,
+        in_specs=[VMEM] * len(near) + [HBM] * len(far),
+        out_specs=[VMEM] * len(held),
+        scratch_shapes=[
+            *[pltpu.VMEM(o.shape, o.dtype) for o in far],
+            pltpu.SemaphoreType.DMA((len(far),)),
+        ],
+        compiler_params=params(8),
+        cost_estimate=cost(512 * 64),
+    )(*[in_vmem(o) for o in near], *[in_hbm(o) for o in far])
+    near = [away, *small]
+    state = pl.pallas_call(
+        functools.partial(next_kernel, counts, ((2, 1), (3, 1))),
+        out_shape=held,
+        in_specs=[VMEM] * (len(near) + len(held)),
+        out_specs=[VMEM] * len(held),
+        input_output_aliases={len(near) + i: i for i in range(len(held))},
+        compiler_params=params(8),
+        cost_estimate=cost(256 * 64),
+    )(*[in_vmem(o) for o in near], *[in_vmem(o) for o in state])
+    near = [last, *small]
+    far = [out_gain, out_bias]
+    return pl.pallas_call(
+        functools.partial(last_kernel, counts, ((2, 0), (3, 0))),
+        out_shape=jax.ShapeDtypeStruct((size, length // chan_count, c), jnp.bfloat16),
+        in_specs=[VMEM] * (len(near) + len(held)) + [HBM] * len(far),
+        out_specs=VMEM,
+        scratch_shapes=[
+            pltpu.VMEM((length, size * sub_count, h), jnp.float32),
+            pltpu.VMEM((length, length // chan_count, h), jnp.float32),
+            pltpu.VMEM((length, length // chan_count, h), jnp.bfloat16),
+            *[pltpu.VMEM(o.shape, o.dtype) for o in far],
+            pltpu.SemaphoreType.DMA((len(far),)),
+        ],
+        compiler_params=params(16),
+        cost_estimate=cost(1024),
+    )(*[in_vmem(o) for o in near], *[in_vmem(o) for o in state], *[in_hbm(o) for o in far])
+
+
 def solution(mesh):
+    def body(pair, *rest):
+        size, length, c = pair.shape
+        small = 2 * length * length * c <= GATHER_LIMIT
+        fits = mesh.shape["sub"] == 2 and mesh.shape["rows"] == 4 and size * 2 == 8
+        chans = mesh.shape["chan"]
+        if not (small and fits and chans & (chans - 1) == 0):
+            return shards(pair, *rest)
+        return gathered(pair, *rest)
+
     placed = (
         P(("crops", "rows", "sub"), None, None),
         P("crops"),
@@ -96,7 +428,7 @@
         P(),
     )
     return jax.shard_map(
-        shards,
+        body,
         mesh=mesh,
         in_specs=placed,
         out_specs=P(("crops", "rows", "sub"), "chan", None),

time: 74.4 us -> 20 us (0.27)
  blocking collectives: 35 us -> 0 us
  local copies, waits for them, and re-layouts: 7.84 us -> 0.02 us
  starting transfers between devices: 14.5 us -> 7.32 us
  Pallas kernels: 0 us -> 6.41 us
  waiting for transfers between devices: 11.4 us -> 5.99 us
  other arithmetic: 2.48 us -> 0 us
  matrix products: 2.32 us -> 0 us
    all_gather x3 -> x0, blocking collectives: 35 us -> none  [the longest x1 15.9 us: shards(): lax.all_gather(right_edges, ('rows', 'sub'), axis=1, tiled=True)]
    all_to_all x4 -> x0, starting transfers between devices: 14.5 us -> none  [the longest x2 6.47 us: finish(): lax.all_to_all(triangle, 'chan', split_axis=2, concat_axis=0, tiled=True)]
    all_to_all x4 -> x0, waiting for transfers between devices: 11.4 us -> none  [the longest x2 6.63 us: finish(): lax.all_to_all(triangle, 'chan', split_axis=2, concat_axis=0, tiled=True)]
    ppermute x0 -> x6, starting transfers between devices: none -> 7.32 us  [the longest x5 6.58 us: swap(): return lax.ppermute(value, axis, [(i, i ^ step) for i in range(count)])]
    pallas_call x0 -> x4, Pallas kernels: none -> 6.41 us  [the longest x1 3.78 us: gathered(): pl.pallas_call(functools.partial(last_kernel, counts, ((2, 0), (3, 0))),...]
    ppermute x0 -> x6, waiting for transfers between devices: none -> 5.99 us  [the longest x5 3.92 us: swap(): return lax.ppermute(value, axis, [(i, i ^ step) for i in range(count)])]
    unnamed x26 -> x8, local copies, waits for them, and re-layouts: 5.09 us -> 0.02 us
    dot_general x8 -> x0, matrix products: 2.32 us -> none  [the longest x2 0.87 us: finish(): jnp.einsum('hij,hc->ijc', scaled, out_weight[layer_index], preferred_elem...]
  transfers between devices with their start and end apart: 4 -> 6, of which waited for: 3 -> 2; matrix products, arithmetic and copies ran while one was open for 3% -> 0% of each run, Pallas kernels for 0% -> 13%
where the time goes in v1:
time: 20 us; the launch traced here: 19.8 us
  starting transfers between devices  7.32 us (37%)
  Pallas kernels  6.41 us (32%)
  waiting for transfers between devices  5.99 us (30%)
    ppermute x5, starting transfers between devices, swap(): return lax.ppermute(value, axis, [(i, i ^ step) for i in range(count)])  6.58 us
    ppermute x5, waiting for transfers between devices, swap(): return lax.ppermute(value, axis, [(i, i ^ step) for i in range(count)])  3.92 us
    pallas_call x1, Pallas kernels, gathered(): pl.pallas_call(functools.partial(last_kernel, counts, ((2, 0), (3, 0))),...  3.78 us
    ppermute x1, waiting for transfers between devices, gathered(): first = lax.ppermute(pair, ('rows', 'sub'), cross)  2.08 us
    pallas_call x1, Pallas kernels, gathered(): pl.pallas_call(functools.partial(first_kernel, counts, ((0, 1), (1, 1), (...  1.96 us
    ppermute x1, starting transfers between devices, gathered(): first = lax.ppermute(pair, ('rows', 'sub'), cross)  0.74 us
    pallas_call x1, Pallas kernels, gathered(): pl.pallas_call(functools.partial(next_kernel, counts, ((2, 1), (3, 1))),...  0.67 us
  transfers between devices with their start and end apart: 6, of which 2 were waited for; matrix products, arithmetic and copies ran while one was open for 0% of the time, Pallas kernels for 13%

profile of v1, /device:TPU:0, one launch (start us, length us, event | category | flops | bytes accessed | tf_op | source)
XLA Modules:
  0.0 19.8 jit_solution(17494525821660883199)
XLA Ops:
  0.0 0.0 copy-start.2
  0.0 3.0 %collective-permute-start.5 = (bf16[2,4,64,128]{3,2,1,0:T(8,128)(2,1)}, bf16[2,4,64,128]{3,2,1,0:T(8,128)(2,1)S(1)}, u32[]{:S(2)}, u32[]{:S(2)}) collective-permute-start(bf16[2,4,64,128]{3,2,1,0:T(8,128)(2,1)} %bitcast.2), channel_id=1, source_target_pairs={{0,2},{2,0},{1,3},{3,1},{4,6},{6,4},{5,7},{7,5},{8,10},{10,8},{9,1... | collective-permute-start | bytes 393224 | tf_op jit(solution)/shard_map/ppermute | solution.py:96
  3.0 0.7 %collective-permute-start.1 = (bf16[4,32,128]{2,1,0:T(8,128)(2,1)}, bf16[4,32,128]{2,1,0:T(8,128)(2,1)S(1)}, u32[]{:S(2)}, u32[]{:S(2)}) collective-permute-start(bf16[4,32,128]{2,1,0:T(8,128)(2,1)} %refs_8_.1), channel_id=1, source_target_pairs={{0,5},{1,4},{4,1},{5,0},{8,13},{9,12},{12,9},{13,8},{2,7},{3,6},{6... | collective-permute-start | bytes 98312 | tf_op jit(solution)/shard_map/ppermute | solution.py:338
  3.7 1.0 %collective-permute-start = (bf16[4,32,128]{2,1,0:T(8,128)(2,1)}, bf16[4,32,128]{2,1,0:T(8,128)(2,1)S(1)}, u32[]{:S(2)}, u32[]{:S(2)}) collective-permute-start(bf16[4,32,128]{2,1,0:T(8,128)(2,1)} %refs_8_.1), channel_id=1, source_target_pairs={{0,1},{1,0},{2,3},{3,2},{4,5},{5,4},{6,7},{7,6},{8,9},{9,8},{10,11... | collective-permute-start | bytes 98312 | tf_op jit(solution)/shard_map/ppermute | solution.py:96
  4.7 2.1 %collective-permute-done.1.b_ref.refs_1_ = bf16[4,32,128]{2,1,0:T(8,128)(2,1)S(1)} collective-permute-done((bf16[4,32,128]{2,1,0:T(8,128)(2,1)}, bf16[4,32,128]{2,1,0:T(8,128)(2,1)S(1)}, u32[]{:S(2)}, u32[]{:S(2)}) %collective-permute-start.1) | collective-permute-done | bytes 32800 | tf_op jit(solution)/shard_map/ppermute | solution.py:338
  6.7 0.0 collective-permute-done.a_ref.refs_0_
  6.7 0.0 copy-start.1
  6.8 0.0 copy-start
  6.8 0.0 copy-start.3
  6.8 2.7 %collective-permute-start.2 = (bf16[8,32,128]{2,1,0:T(8,128)(2,1)S(1)}, bf16[8,32,128]{2,1,0:T(8,128)(2,1)S(1)}, u32[]{:S(2)}, u32[]{:S(2)}) collective-permute-start(bf16[8,32,128]{2,1,0:T(8,128)(2,1)S(1)} %shard_map.91), channel_id=1, source_target_pairs={{0,8},{4,12},{8,0},{12,4},{1,9},{5,13},{9,1},{13,5},{2,10},{6,14},... | collective-permute-start | bytes 196616 | tf_op jit(solution)/shard_map/ppermute | solution.py:96
  9.4 0.0 collective-permute-start.4
  9.4 3.9 %collective-permute-done.2.block_ref = bf16[8,32,128]{2,1,0:T(8,128)(2,1)S(1)} collective-permute-done((bf16[8,32,128]{2,1,0:T(8,128)(2,1)S(1)}, bf16[8,32,128]{2,1,0:T(8,128)(2,1)S(1)}, u32[]{:S(2)}, u32[]{:S(2)}) %collective-permute-start.2) | collective-permute-done | bytes 65568 | tf_op jit(solution)/shard_map/ppermute | solution.py:96
  13.3 0.0 collective-permute-start.3
  13.3 0.0 collective-permute-done.4.refs_2_
  13.3 0.0 collective-permute-done.5.refs_4_
  13.4 0.0 copy-done.2
  13.4 0.0 copy-done.1
  13.4 0.0 copy-done
  13.4 0.0 copy-done.3
  13.4 2.0 %shard_map.92 = (f32[32,32,128]{2,1,0:T(8,128)S(1)}, f32[32,32,128]{2,1,0:T(8,128)S(1)}, f32[32,32,128]{2,1,0:T(8,128)S(1)}, f32[32,32,128]{2,1,0:T(8,128)S(1)},...) custom-call(bf16[4,32,128]{2,1,0:T(8,128)(2,1)S(1)} %collective-perm, ...), custom_call_target="tpu_custom_call" | custom-call | flops 8589934592 | tf_op jit(solution)/shard_map/pallas_call | solution.py:368
  15.4 0.7 %shard_map.93 = (f32[32,32,128]{2,1,0:T(8,128)S(1)}, f32[32,32,128]{2,1,0:T(8,128)S(1)}, f32[32,32,128]{2,1,0:T(8,128)S(1)}, f32[32,32,128]{2,1,0:T(8,128)S(1)},...) custom-call(bf16[8,32,128]{2,1,0:T(8,128)(2,1)S(1)} %collective-perm, ...), custom_call_target="tpu_custom_call", output_to_operand_aliasing={{0}: (3, {}), {1}: (4, {}), {2}: (5, {}), {3}: (6, {}), {4}... | custom-call | flops 4294967296 | tf_op jit(solution)/shard_map/pallas_call | solution.py:381
  16.0 0.0 collective-permute-done.3.block_ref
  16.1 3.8 %shard_map.94 = bf16[4,16,128]{2,1,0:T(8,128)(2,1)} custom-call(bf16[8,32,128]{2,1,0:T(8,128)(2,1)S(1)} %collective-permute-done.3.block_ref, f32[2,128]{1,0:T(2,128)S(1)} %copy-done, f32[2,128]{1,0:T(2,128)S(1)} %copy-done.1, f32[32,32,128]{2,1,0:T(8,128)S(1)} %get-tuple-element.35.refs_0_, f32[32,32,128]{2,1,0:T(8,128)S(1)} %get-tuple-element.36.refs_1_, ...), custom_call_target="tpu_custom_call" | custom-call | flops 268435456 | tf_op jit(solution)/shard_map/pallas_call | solution.py:392
  (1 shorter events, 0.0 us)
Async XLA Ops:
  0.0 13.4 %copy-start.2 = (bf16[2,4,128,64]{2,3,1,0:T(8,128)(2,1)S(1)}, bf16[2,4,128,64]{2,3,1,0:T(8,128)(2,1)}, u32[]{:S(2)}) copy-start(bf16[2,4,128,64]{2,3,1,0:T(8,128)(2,1)} %param.13) | copy-start | bytes 393220
  0.0 13.3 %collective-permute-start.5 = (bf16[2,4,64,128]{3,2,1,0:T(8,128)(2,1)}, bf16[2,4,64,128]{3,2,1,0:T(8,128)(2,1)S(1)}, u32[]{:S(2)}, u32[]{:S(2)}) collective-permute-start(bf16[2,4,64,128]{3,2,1,0:T(8,128)(2,1)} %bitcast.2), channel_id=1, source_target_pairs={{0,2},{2,0},{1,3},{3,1},{4,6},{6,4},{5,7},{7,5},{8,10},{10,8},{9,1... | collective-permute-start | bytes 393224 | tf_op jit(solution)/shard_map/ppermute | solution.py:96
  3.0 3.8 %collective-permute-start.1 = (bf16[4,32,128]{2,1,0:T(8,128)(2,1)}, bf16[4,32,128]{2,1,0:T(8,128)(2,1)S(1)}, u32[]{:S(2)}, u32[]{:S(2)}) collective-permute-start(bf16[4,32,128]{2,1,0:T(8,128)(2,1)} %refs_8_.1), channel_id=1, source_target_pairs={{0,5},{1,4},{4,1},{5,0},{8,13},{9,12},{12,9},{13,8},{2,7},{3,6},{6... | collective-permute-start | bytes 98312 | tf_op jit(solution)/shard_map/ppermute | solution.py:338
  3.7 3.0 %collective-permute-start = (bf16[4,32,128]{2,1,0:T(8,128)(2,1)}, bf16[4,32,128]{2,1,0:T(8,128)(2,1)S(1)}, u32[]{:S(2)}, u32[]{:S(2)}) collective-permute-start(bf16[4,32,128]{2,1,0:T(8,128)(2,1)} %refs_8_.1), channel_id=1, source_target_pairs={{0,1},{1,0},{2,3},{3,2},{4,5},{5,4},{6,7},{7,6},{8,9},{9,8},{10,11... | collective-permute-start | bytes 98312 | tf_op jit(solution)/shard_map/ppermute | solution.py:96
  6.7 6.6 %copy-start.1 = (f32[2,128]{1,0:T(2,128)S(1)}, f32[2,128]{1,0:T(2,128)}, u32[]{:S(2)}) copy-start(f32[2,128]{1,0:T(2,128)} %ib_ref.3) | copy-start | bytes 3076
  6.8 6.6 %copy-start = (f32[2,128]{1,0:T(2,128)S(1)}, f32[2,128]{1,0:T(2,128)}, u32[]{:S(2)}) copy-start(f32[2,128]{1,0:T(2,128)} %ig_ref.3) | copy-start | bytes 3076
  6.8 6.6 %copy-start.3 = (s32[32]{0:T(128)S(1)}, s32[32]{0:T(128)}, u32[]{:S(2)}) copy-start(s32[32]{0:T(128)} %param.10) | copy-start | bytes 388
  6.8 6.6 %collective-permute-start.2 = (bf16[8,32,128]{2,1,0:T(8,128)(2,1)S(1)}, bf16[8,32,128]{2,1,0:T(8,128)(2,1)S(1)}, u32[]{:S(2)}, u32[]{:S(2)}) collective-permute-start(bf16[8,32,128]{2,1,0:T(8,128)(2,1)S(1)} %shard_map.91), channel_id=1, source_target_pairs={{0,8},{4,12},{8,0},{12,4},{1,9},{5,13},{9,1},{13,5},{2,10},{6,14},... | collective-permute-start | bytes 196616 | tf_op jit(solution)/shard_map/ppermute | solution.py:96
  9.4 3.9 %collective-permute-start.4 = (bf16[4,32,128]{2,1,0:T(8,128)(2,1)S(1)}, bf16[4,32,128]{2,1,0:T(8,128)(2,1)S(1)}, u32[]{:S(2)}, u32[]{:S(2)}) collective-permute-start(bf16[4,32,128]{2,1,0:T(8,128)(2,1)S(1)} %collective-permute-done.1.b_ref.refs_1_), channel_id=1, source_target_pairs={{0,1},{1,0},{2,3},{3,2},{4,5},{5,4},{6,7},{7,6},{8,9},{9,8},{10,11... | collective-permute-start | bytes 98312 | tf_op jit(solution)/shard_map/ppermute | solution.py:96
  13.3 2.7 %collective-permute-start.3 = (bf16[8,32,128]{2,1,0:T(8,128)(2,1)S(1)}, bf16[8,32,128]{2,1,0:T(8,128)(2,1)S(1)}, u32[]{:S(2)}, u32[]{:S(2)}) collective-permute-start(bf16[8,32,128]{2,1,0:T(8,128)(2,1)S(1)} %collective-permute-done.2.block_ref), channel_id=1, source_target_pairs={{0,1},{1,0},{2,3},{3,2},{4,5},{5,4},{6,7},{7,6},{8,9},{9,8},{10,11... | collective-permute-start | bytes 196616 | tf_op jit(solution)/shard_map/ppermute | solution.py:96

commit v2 on v0

--- a/solution.py
+++ b/solution.py
@@ -1,9 +1,17 @@
+import functools
+
 import jax
 import jax.numpy as jnp
 from jax import lax
+from jax.experimental import pallas as pl
+from jax.experimental.pallas import tpu as pltpu
 from jax.sharding import PartitionSpec as P
 
+
 epsilon = 1e-05
+
+
+GATHER_LIMIT = 1 << 20
 
 
 def normalize(values, reduce_axis):
@@ -83,7 +91,332 @@
     return finish(triangle.astype(jnp.bfloat16), normed, layer_one, 1)
 
 
+def swap(value, axis, step):
+    count = lax.axis_size(axis)
+    return lax.ppermute(value, axis, [(i, i ^ step) for i in range(count)])
+
+
+def mm(a, b):
+    return jnp.dot(a, b, preferred_element_type=jnp.float32)
+
+
+def mmt(a, b):
+    return lax.dot_general(a, b, (((1,), (1,)), ((), ())), preferred_element_type=jnp.float32)
+
+
+def constants(c):
+    average = jnp.full((c, c), 1.0 / c, jnp.float32)
+    diagonal = lax.broadcasted_iota(jnp.int32, (c, c), 0) == lax.broadcasted_iota(jnp.int32, (c, c), 1)
+    centring = jnp.where(diagonal, 1.0 - 1.0 / c, -1.0 / c)
+    return centring.astype(jnp.bfloat16), average.astype(jnp.bfloat16)
+
+
+def layer_norm(values, gain, bias, centring, average):
+    centred = mm(values, centring)
+    spread = mm((centred * centred).astype(jnp.bfloat16), average)
+    return (centred * lax.rsqrt(spread + epsilon) * gain + bias).astype(jnp.bfloat16)
+
+
+def gated(half_gate, half_value):
+    return half_value * jnp.tanh(half_gate) + half_value
+
+
+class Stage:
+    def __init__(self, counts, state, small):
+        (self.left, self.right, self.turned, self.gate, self.x, self.tri, self.w, self.mask, self.gw, self.ow) = state
+        self.ig, self.ib = small
+        self.rows_count, self.chan_count, self.sub_count, self.size = counts
+        self.row = lax.axis_index("rows")
+        self.chan = lax.axis_index("chan")
+        self.sub = lax.axis_index("sub")
+        self.length, _, self.c = self.x.shape
+        self.h = self.mask.shape[1]
+        self.chip = self.size * self.sub_count
+        self.quarter = self.length // self.chan_count
+        self.centring, self.average = constants(self.c)
+
+    def at(self, rs, ss):
+        return ((self.row ^ rs) * self.sub_count + (self.sub ^ ss)) * self.size
+
+    def halves(self, ss):
+        return [
+            self.chan * self.quarter + i * self.chip + (self.sub ^ ss) * self.size
+            for i in range(self.quarter // self.chip)
+        ]
+
+    def slots(self):
+        return [[self.at(0, 0) - self.sub * self.size + i * self.size for i in range(self.sub_count)],
+                self.halves(0), self.halves(1)]
+
+    def norm(self, x, layer):
+        return layer_norm(x, self.ig[layer:layer + 1], self.ib[layer:layer + 1], self.centring, self.average)
+
+    def keep(self, step, ref):
+        part = self.h // self.chan_count
+        at = pl.multiple_of((self.chan ^ step) * part, part)
+        self.w[:, :, pl.ds(at, part), :] = ref[...] * jnp.bfloat16(0.5)
+
+    def places(self, where):
+        return [pl.ds(self.at(*w), self.size) for w in where]
+
+    def part(self, value, i):
+        area = self.size * self.length
+        return value[i * area:(i + 1) * area].reshape(self.size, self.length, value.shape[1])
+
+    def enter(self, where, blocks):
+        area = self.size * self.length
+        x = jnp.concatenate([b.reshape(area, self.c) for b in blocks], 0)
+        normed = self.norm(x, 0)
+        g = jnp.tanh(mm(normed, self.gw[0]))
+        for i, place in enumerate(self.places(where)):
+            self.gate[place] = self.part(g, i)
+            self.x[place] = self.part(x.astype(jnp.float32), i)
+        return normed
+
+    def edges(self, where, normed):
+        places = self.places(where)
+        both = [self.mask[p][:, None, :] * self.mask[...][None] for p in places]
+        for ref, q in ((self.left, 0), (self.right, 2)):
+            p = mmt(normed, self.w[0, q:q + 2].reshape(2 * self.h, self.c))
+            for i, place in enumerate(places):
+                ref[place] = gated(self.part(p[:, :self.h], i), self.part(p[:, self.h:], i) * both[i])
+
+    def turn(self, slot):
+        rows = jnp.concatenate([self.right[pl.ds(o, self.size)] for o in self.slots()[slot]], 0)
+        self.turned[slot] = jnp.swapaxes(rows, 0, 1)
+
+    def triangle(self, ks, slots):
+        def inner(m, acc):
+            rs = [self.turned[t, m] for t in slots]
+            out = []
+            for i, k in enumerate(ks):
+                l = self.left[k, pl.ds(m, 1), :]
+                out += [acc[i * len(rs) + j] + l * r for j, r in enumerate(rs)]
+            return tuple(out)
+
+        zero = tuple(jnp.zeros((self.chip, self.h), jnp.float32) for _ in range(len(ks) * len(slots)))
+        acc = lax.fori_loop(0, self.length, inner, zero, unroll=8)
+        for i, k in enumerate(ks):
+            for j, t in enumerate(slots):
+                self.tri[t, k] = acc[i * len(slots) + j]
+
+    def block_rows(self, places):
+        return [self.at(*p) + i for p in places for i in range(self.size)]
+
+    def columns(self, ref, slot):
+        return jnp.concatenate([ref[:, pl.ds(o, self.size), :] for o in self.slots()[slot]], 1)
+
+    def mask_rows(self, slot):
+        return jnp.concatenate([self.mask[pl.ds(o, self.size)] for o in self.slots()[slot]], 0)
+
+
+def early_kernel(counts, *refs):
+    mask_ref, ig_ref, ib_ref, pair_hbm, w_hbm, gw_hbm, ow_hbm = refs[:7]
+    gate, x, w, mask, gw, ow, normed = refs[7:14]
+    raw, sems = refs[14:18], refs[18]
+    copies = [pltpu.make_async_copy(a, b, sems.at[i]) for i, (a, b) in enumerate(zip((pair_hbm, w_hbm, gw_hbm, ow_hbm), raw))]
+    for copy in copies:
+        copy.start()
+    s = Stage(counts, (mask, None, None, gate, x, None, w, mask, gw, ow), (ig_ref, ib_ref))
+    half = jnp.bfloat16(0.5)
+    across = mask_ref[...].astype(jnp.float32)
+    square = (s.length, s.length)
+    diagonal = lax.broadcasted_iota(jnp.int32, square, 0) == lax.broadcasted_iota(jnp.int32, square, 1)
+    mask[...] = mm(jnp.where(diagonal, across, 0.0).astype(jnp.bfloat16), jnp.ones((s.length, s.h), jnp.bfloat16))
+    for copy in copies:
+        copy.wait()
+    pair_ref, w_ref, gw_ref, ow_ref = raw
+    gw[...] = gw_ref[...] * half
+    ow[...] = ow_ref[...] * half
+    s.keep(0, w_ref)
+    normed[...] = s.enter(((0, 0),), (pair_ref[...],))
+
+
+def first_kernel(counts, where, *refs):
+    n = len(where) - 1
+    others = counts[1] - 1
+    blocks, weights = refs[:n], refs[n:n + others]
+    ig_ref, ib_ref, normed_ref, mask_in, gw_in = refs[n + others:n + others + 5]
+    left, right, turned, tri, gate, x, w = refs[n + others + 8:]
+    s = Stage(counts, (left, right, turned, gate, x, tri, w, mask_in, gw_in, None), (ig_ref, ib_ref))
+    for i, ref in enumerate(weights):
+        s.keep(i + 1, ref)
+    normed = s.enter(where[1:], [b[...] for b in blocks])
+    s.edges(where, jnp.concatenate([normed_ref[...], normed], 0))
+    s.turn(0)
+    s.turn(1)
+    ks = s.block_rows(where)
+    middle = len(ks) // 2
+    s.triangle(ks[:middle], (0, 1))
+    s.triangle(ks[middle:], (0, 1))
+
+
+def last_kernel(counts, where, *refs):
+    n = len(where)
+    blocks = refs[:n]
+    ig_ref, ib_ref = refs[n:n + 2]
+    state = refs[n + 2:n + 12]
+    og_hbm, ob_hbm, out_ref, z_ref, l1_ref, r1_ref, og_ref, ob_ref, sems = refs[n + 12:]
+    copies = [pltpu.make_async_copy(og_hbm, og_ref, sems.at[0]), pltpu.make_async_copy(ob_hbm, ob_ref, sems.at[1])]
+    for copy in copies:
+        copy.start()
+    s = Stage(counts, state, (ig_ref, ib_ref))
+    size, length, c, h, chip, quarter = s.size, s.length, s.c, s.h, s.chip, s.quarter
+    s.edges(where, s.enter(where, [b[...] for b in blocks]))
+    s.turn(2)
+    s.triangle(s.block_rows(where), (0, 1))
+    middle = length // 2
+    s.triangle(range(middle), (2,))
+    s.triangle(range(middle, length), (2,))
+    for copy in copies:
+        copy.wait()
+
+    def finish(tri, half_gate, residual, layer):
+        scaled = layer_norm(
+            tri.astype(jnp.bfloat16), og_ref[layer:layer + 1], ob_ref[layer:layer + 1], s.centring, s.average
+        )
+        update = mm(scaled, s.ow[layer])
+        return (residual + (update * half_gate + update)).astype(jnp.bfloat16)
+
+    area = length * chip
+    half_gate = jnp.concatenate([s.columns(s.gate, t).reshape(area, c) for t in range(3)], 0)
+    residual = jnp.concatenate([s.columns(s.x, t).reshape(area, c) for t in range(3)], 0)
+    z = finish(s.tri[...].reshape(3 * area, h), half_gate, residual, 0)
+    z_ref[...] = z.astype(jnp.float32).reshape(3, length, chip, c)
+
+    mask = s.mask[...][:, None, :]
+    normed = s.norm(z, 1)
+    shape = (length, chip, h)
+    p = mmt(normed[:area], s.w[1, 0:2].reshape(2 * h, c))
+    l1_ref[...] = gated(p[:, :h].reshape(shape), p[:, h:].reshape(shape) * (mask * s.mask_rows(0)[None]))
+    p = mmt(normed[area:], s.w[1, 2:4].reshape(2 * h, c))
+    for t in (1, 2):
+        at = slice((t - 1) * area, t * area)
+        r1_ref[t - 1] = gated(p[at, :h].reshape(shape), p[at, h:].reshape(shape) * (mask * s.mask_rows(t)[None]))
+    own = s.at(0, 0)
+    mine = z_ref[1:3, pl.ds(own, size)].reshape(2 * size * chip, c)
+    half_gate = jnp.tanh(mm(s.norm(mine.astype(jnp.bfloat16), 1), s.gw[1]))
+
+    first = s.sub * size
+
+    def inner(k, acc):
+        rs = [r1_ref[t, k] for t in range(2)]
+        ls = [l1_ref[k, pl.ds(first + i, 1), :] for i in range(size)]
+        return tuple(acc[t * size + i] + ls[i] * rs[t] for t in range(2) for i in range(size))
+
+    zero = tuple(jnp.zeros((chip, h), jnp.float32) for _ in range(2 * size))
+    tri = jnp.concatenate(lax.fori_loop(0, length, inner, zero, unroll=8), 0)
+    z = finish(tri, half_gate, mine, 1).astype(jnp.float32).reshape(2, size, chip, c)
+    even = jnp.where(s.sub == 0, z[0], z[1])
+    odd = jnp.where(s.sub == 0, z[1], z[0])
+    rows = [v[:, i * size:(i + 1) * size] for i in range(quarter // chip) for v in (even, odd)]
+    out_ref[...] = jnp.concatenate(rows, 1).astype(jnp.bfloat16)
+
+
+def in_vmem(value):
+    return pltpu.with_memory_space_constraint(value, pltpu.VMEM)
+
+
+def in_hbm(value):
+    return pltpu.with_memory_space_constraint(value, pltpu.HBM)
+
+
+VMEM = pl.BlockSpec(memory_space=pltpu.VMEM)
+HBM = pl.BlockSpec(memory_space=pltpu.HBM)
+
+
+def gathered(
+    pair, residue_mask, in_gain, in_bias, projections, gate_weight, out_gain, out_bias, out_weight
+):
+    rows_count, chan_count, sub_count = (lax.axis_size(a) for a in ("rows", "chan", "sub"))
+    size, length, c = pair.shape
+    h = out_weight.shape[1]
+    counts = (rows_count, chan_count, sub_count, size)
+    turned = jnp.swapaxes(projections, 2, 3)
+    hops = tuple(range(1, rows_count))
+    far, near = {}, {}
+    for rs in hops:
+        far[rs] = swap(pair, "rows", rs)
+    near[0] = swap(pair, "sub", 1)
+    weights = [swap(turned, "chan", i) for i in range(1, chan_count)]
+    for rs in hops:
+        near[rs] = swap(far[rs], "sub", 1)
+
+    wide = pltpu.VMEM((length, length, c), jnp.float32)
+    tiles = pltpu.VMEM((3, length, size * sub_count, h), jnp.float32)
+    small = [residue_mask[None], in_gain, in_bias]
+
+    def call(kernel, near, far, out_shape, scratch=(), aliases={}, rows=0, mib=8):
+        return pl.pallas_call(
+            kernel,
+            out_shape=out_shape,
+            in_specs=[VMEM] * len(near) + [HBM] * len(far),
+            out_specs=jax.tree.map(lambda _: VMEM, out_shape),
+            scratch_shapes=[
+                *scratch,
+                *[pltpu.VMEM(o.shape, o.dtype) for o in far],
+                *([pltpu.SemaphoreType.DMA((len(far),))] if far else []),
+            ],
+            input_output_aliases=aliases,
+            compiler_params=pltpu.CompilerParams(vmem_limit_bytes=mib << 20),
+            cost_estimate=pl.CostEstimate(flops=rows * c * c * 16, bytes_accessed=0, transcendentals=0),
+        )(*[in_vmem(o) for o in near], *[in_hbm(o) for o in far])
+
+    gate, x, w, mask, gw, ow, normed = call(
+        functools.partial(early_kernel, counts),
+        small,
+        [pair, turned, gate_weight, out_weight],
+        [
+            wide,
+            wide,
+            pltpu.VMEM((2, 4, h, c), jnp.bfloat16),
+            pltpu.VMEM((length, h), jnp.float32),
+            pltpu.VMEM((2, c, c), jnp.bfloat16),
+            pltpu.VMEM((2, h, c), jnp.bfloat16),
+            pltpu.VMEM((size * length, c), jnp.bfloat16),
+        ],
+        rows=length * length,
+    )
+    where = ((0, 0), (0, 1), *[(rs, 0) for rs in hops])
+    near_one = [near[0], *[far[rs] for rs in hops], *weights, in_gain, in_bias, normed, mask, gw, gate, x, w]
+    left, right, folded, tri, gate, x, w = call(
+        functools.partial(first_kernel, counts, where),
+        near_one,
+        [],
+        [wide, wide, tiles, tiles, wide, wide, pltpu.VMEM(w.shape, w.dtype)],
+        aliases={len(near_one) - 3 + i: 4 + i for i in range(3)},
+        rows=length * length,
+    )
+    state = [left, right, folded, gate, x, tri, w, mask, gw, ow]
+    return call(
+        functools.partial(last_kernel, counts, tuple((rs, 1) for rs in hops)),
+        [*[near[rs] for rs in hops], in_gain, in_bias, *state],
+        [out_gain, out_bias],
+        jax.ShapeDtypeStruct((size, length // chan_count, c), jnp.bfloat16),
+        scratch=[
+            pltpu.VMEM((3, length, size * sub_count, c), jnp.float32),
+            pltpu.VMEM((length, size * sub_count, h), jnp.float32),
+            pltpu.VMEM((2, length, size * sub_count, h), jnp.float32),
+        ],
+        rows=1,
+        mib=16,
+    )
+
+
 def solution(mesh):
+    def body(pair, *rest):
+        size, length, c = pair.shape
+        small = 2 * length * length * c <= GATHER_LIMIT
+        fits = (
+            mesh.shape["sub"] == 2
+            and mesh.shape["rows"] & (mesh.shape["rows"] - 1) == 0
+            and size * 2 == 8
+            and length == 16 * mesh.shape["chan"]
+        )
+        if not (small and fits):
+            return shards(pair, *rest)
+        return gathered(pair, *rest)
+
     placed = (
         P(("crops", "rows", "sub"), None, None),
         P("crops"),
@@ -95,10 +428,13 @@
         P(),
         P(),
     )
-    return jax.shard_map(
-        shards,
+    step = jax.shard_map(
+        body,
         mesh=mesh,
         in_specs=placed,
         out_specs=P(("crops", "rows", "sub"), "chan", None),
         check_vma=False,
     )
+    if 8 * mesh.shape["rows"] != 16 * mesh.shape["chan"]:
+        return step
+    return step

time: 74.4 us -> 19.3 us (0.26)
  blocking collectives: 35 us -> 0 us
  local copies, waits for them, and re-layouts: 7.84 us -> 0.01 us
  starting transfers between devices: 14.5 us -> 7.94 us
  waiting for transfers between devices: 11.4 us -> 5.2 us
  Pallas kernels: 0 us -> 5.88 us
  other arithmetic: 2.48 us -> 0 us
  matrix products: 2.32 us -> 0 us
    all_gather x3 -> x0, blocking collectives: 35 us -> none  [the longest x1 15.9 us: shards(): lax.all_gather(right_edges, ('rows', 'sub'), axis=1, tiled=True)]
    all_to_all x4 -> x0, starting transfers between devices: 14.5 us -> none  [the longest x2 6.47 us: finish(): lax.all_to_all(triangle, 'chan', split_axis=2, concat_axis=0, tiled=True)]
    all_to_all x4 -> x0, waiting for transfers between devices: 11.4 us -> none  [the longest x2 6.63 us: finish(): lax.all_to_all(triangle, 'chan', split_axis=2, concat_axis=0, tiled=True)]
    ppermute x0 -> x8, starting transfers between devices: none -> 7.94 us  [swap(): return lax.ppermute(value, axis, [(i, i ^ step) for i in range(count)])]
    pallas_call x0 -> x3, Pallas kernels: none -> 5.88 us  [call(): pl.pallas_call(kernel, out_shape=out_shape, in_specs=[VMEM] * len(near) +...]
    ppermute x0 -> x8, waiting for transfers between devices: none -> 5.2 us  [swap(): return lax.ppermute(value, axis, [(i, i ^ step) for i in range(count)])]
    unnamed x26 -> x6, local copies, waits for them, and re-layouts: 5.09 us -> 0.01 us
    dot_general x8 -> x0, matrix products: 2.32 us -> none  [the longest x2 0.87 us: finish(): jnp.einsum('hij,hc->ijc', scaled, out_weight[layer_index], preferred_elem...]
  transfers between devices with their start and end apart: 4 -> 8, of which waited for: 3 -> 2; matrix products, arithmetic and copies ran while one was open for 3% -> 0% of each run, Pallas kernels for 0% -> 13%
where the time goes in v2:
time: 19.3 us; the launch traced here: 19.1 us
  starting transfers between devices  7.94 us (41%)
  Pallas kernels  5.88 us (30%)
  waiting for transfers between devices  5.2 us (27%)
    ppermute x8, starting transfers between devices, swap(): return lax.ppermute(value, axis, [(i, i ^ step) for i in range(count)])  7.94 us
    pallas_call x3, Pallas kernels, call(): pl.pallas_call(kernel, out_shape=out_shape, in_specs=[VMEM] * len(near) +...  5.88 us
    ppermute x8, waiting for transfers between devices, swap(): return lax.ppermute(value, axis, [(i, i ^ step) for i in range(count)])  5.2 us
  transfers between devices with their start and end apart: 8, of which 2 were waited for; matrix products, arithmetic and copies ran while one was open for 0% of the time, Pallas kernels for 13%

profile of v2, /device:TPU:0, one launch (start us, length us, event | category | flops | bytes accessed | tf_op | source)
XLA Modules:
  0.0 19.1 jit_solution(2098123498180957793)
XLA Ops:
  0.0 0.0 copy-start.1
  0.0 0.0 copy-start
  0.0 0.0 copy-start.2
  0.0 3.0 %collective-permute-start.7 = (bf16[2,4,64,128]{3,2,1,0:T(8,128)(2,1)}, bf16[2,4,64,128]{3,2,1,0:T(8,128)(2,1)S(1)}, u32[]{:S(2)}, u32[]{:S(2)}) collective-permute-start(bf16[2,4,64,128]{3,2,1,0:T(8,128)(2,1)} %bitcast.3), channel_id=1, source_target_pairs={{0,2},{2,0},{1,3},{3,1},{4,6},{6,4},{5,7},{7,5},{8,10},{10,8},{9,1... | collective-permute-start | bytes 393224 | tf_op jit(solution)/shard_map/ppermute | solution.py:96
  3.0 1.6 %collective-permute-start = (bf16[4,32,128]{2,1,0:T(8,128)(2,1)}, bf16[4,32,128]{2,1,0:T(8,128)(2,1)S(1)}, u32[]{:S(2)}, u32[]{:S(2)}) collective-permute-start(bf16[4,32,128]{2,1,0:T(8,128)(2,1)} %refs_3_.2), channel_id=1, source_target_pairs={{0,4},{4,0},{8,12},{12,8},{1,5},{5,1},{9,13},{13,9},{2,6},{6,2},{1... | collective-permute-start | bytes 98312 | tf_op jit(solution)/shard_map/ppermute | solution.py:96
  4.6 2.6 %collective-permute-start.2 = (bf16[4,32,128]{2,1,0:T(8,128)(2,1)}, bf16[4,32,128]{2,1,0:T(8,128)(2,1)S(1)}, u32[]{:S(2)}, u32[]{:S(2)}) collective-permute-start(bf16[4,32,128]{2,1,0:T(8,128)(2,1)} %refs_3_.2), channel_id=1, source_target_pairs={{0,8},{4,12},{8,0},{12,4},{1,9},{5,13},{9,1},{13,5},{2,10},{6,14},... | collective-permute-start | bytes 98312 | tf_op jit(solution)/shard_map/ppermute | solution.py:96
  7.2 0.2 %collective-permute-start.4 = (bf16[4,32,128]{2,1,0:T(8,128)(2,1)}, bf16[4,32,128]{2,1,0:T(8,128)(2,1)S(1)}, u32[]{:S(2)}, u32[]{:S(2)}) collective-permute-start(bf16[4,32,128]{2,1,0:T(8,128)(2,1)} %refs_3_.2), channel_id=1, source_target_pairs={{0,12},{4,8},{8,4},{12,0},{1,13},{5,9},{9,5},{13,1},{2,14},{6,10},... | collective-permute-start | bytes 98312 | tf_op jit(solution)/shard_map/ppermute | solution.py:96
  7.4 0.0 collective-permute-start.6
  7.4 0.0 collective-permute-done.refs_1_
  7.4 0.5 %collective-permute-start.1 = (bf16[4,32,128]{2,1,0:T(8,128)(2,1)S(1)}, bf16[4,32,128]{2,1,0:T(8,128)(2,1)S(1)}, u32[]{:S(2)}, u32[]{:S(2)}) collective-permute-start(bf16[4,32,128]{2,1,0:T(8,128)(2,1)S(1)} %collective-permute-done.refs_1_), channel_id=1, source_target_pairs={{0,1},{1,0},{2,3},{3,2},{4,5},{5,4},{6,7},{7,6},{8,9},{9,8},{10,11... | collective-permute-start | bytes 98312 | tf_op jit(solution)/shard_map/ppermute | solution.py:96
  7.9 2.0 %collective-permute-done.2.refs_2_ = bf16[4,32,128]{2,1,0:T(8,128)(2,1)S(1)} collective-permute-done((bf16[4,32,128]{2,1,0:T(8,128)(2,1)}, bf16[4,32,128]{2,1,0:T(8,128)(2,1)S(1)}, u32[]{:S(2)}, u32[]{:S(2)}) %collective-permute-start.2) | collective-permute-done | bytes 32800 | tf_op jit(solution)/shard_map/ppermute | solution.py:96
  9.9 0.0 collective-permute-start.3
  9.9 3.2 %collective-permute-done.4.refs_3_ = bf16[4,32,128]{2,1,0:T(8,128)(2,1)S(1)} collective-permute-done((bf16[4,32,128]{2,1,0:T(8,128)(2,1)}, bf16[4,32,128]{2,1,0:T(8,128)(2,1)S(1)}, u32[]{:S(2)}, u32[]{:S(2)}) %collective-permute-start.4) | collective-permute-done | bytes 32800 | tf_op jit(solution)/shard_map/ppermute | solution.py:96
  13.1 0.0 collective-permute-start.5
  13.1 0.0 copy-done.1
  13.1 0.0 copy-done
  13.1 0.0 copy-done.2
  13.2 1.4 %shard_map.91 = (f32[32,32,128]{2,1,0:T(8,128)S(1)}, f32[32,32,128]{2,1,0:T(8,128)S(1)}, bf16[2,4,128,128]{3,2,1,0:T(8,128)(2,1)S(1)}, f32[32,128]{1,0:T(8,128)S...) custom-call(s32[1,32]{1,0:T(1,128)S(1)} %bitcast.2, ...), custom_call_target="tpu_custom_call" | custom-call | flops 268435456 | tf_op jit(solution)/shard_map/pallas_call | solution.py:350
  14.6 0.0 collective-permute-done.6.refs_0_
  14.6 0.0 collective-permute-done.7.refs_4_
  14.6 1.1 %shard_map.92 = (f32[32,32,128]{2,1,0:T(8,128)S(1)}, f32[32,32,128]{2,1,0:T(8,128)S(1)}, f32[3,32,8,128]{3,2,1,0:T(8,128)S(1)}, f32[3,32,8,128]{3,2,1,0:T(8,128)...) custom-call(bf16[4,32,128]{2,1,0:T(8,128)(2,1)S(1)} %collective-perm, ...), custom_call_target="tpu_custom_call", output_to_operand_aliasing={{4}: (10, {}), {5}: (11, {}), {6}: (12, {})} | custom-call | flops 268435456 | tf_op jit(solution)/shard_map/pallas_call | solution.py:350
  15.7 0.0 collective-permute-done.1.refs_0_
  15.7 0.0 collective-permute-done.3.refs_1_
  15.8 0.0 collective-permute-done.5.refs_2_
  15.8 3.3 %shard_map.93 = bf16[4,16,128]{2,1,0:T(8,128)(2,1)} custom-call(bf16[4,32,128]{2,1,0:T(8,128)(2,1)S(1)} %collective-permute-done.1.refs_0_, bf16[4,32,128]{2,1,0:T(8,128)(2,1)S(1)} %collective-permute-done.3.refs_1_, bf16[4,32,128]{2,1,0:T(8,128)(2,1)S(1)} %collective-permute-done.5.refs_2_, f32[2,128]{1,0:T(2,128)S(1)} %copy-done, f32[2,128]{1,0:T(2,128)S(1)} %copy-done.1, ...), custom_call_target="tpu_custom_call" | custom-call | flops 262144 | tf_op jit(solution)/shard_map/pallas_call | solution.py:350
Async XLA Ops:
  0.0 13.1 %copy-start.1 = (f32[2,128]{1,0:T(2,128)S(1)}, f32[2,128]{1,0:T(2,128)}, u32[]{:S(2)}) copy-start(f32[2,128]{1,0:T(2,128)} %refs_4_.1) | copy-start | bytes 3076
  0.0 13.1 %copy-start = (f32[2,128]{1,0:T(2,128)S(1)}, f32[2,128]{1,0:T(2,128)}, u32[]{:S(2)}) copy-start(f32[2,128]{1,0:T(2,128)} %refs_3_.3) | copy-start | bytes 3076
  0.0 13.1 %copy-start.2 = (s32[32]{0:T(128)S(1)}, s32[32]{0:T(128)}, u32[]{:S(2)}) copy-start(s32[32]{0:T(128)} %param.10) | copy-start | bytes 388
  0.0 14.6 %collective-permute-start.7 = (bf16[2,4,64,128]{3,2,1,0:T(8,128)(2,1)}, bf16[2,4,64,128]{3,2,1,0:T(8,128)(2,1)S(1)}, u32[]{:S(2)}, u32[]{:S(2)}) collective-permute-start(bf16[2,4,64,128]{3,2,1,0:T(8,128)(2,1)} %bitcast.3), channel_id=1, source_target_pairs={{0,2},{2,0},{1,3},{3,1},{4,6},{6,4},{5,7},{7,5},{8,10},{10,8},{9,1... | collective-permute-start | bytes 393224 | tf_op jit(solution)/shard_map/ppermute | solution.py:96
  3.0 4.4 %collective-permute-start = (bf16[4,32,128]{2,1,0:T(8,128)(2,1)}, bf16[4,32,128]{2,1,0:T(8,128)(2,1)S(1)}, u32[]{:S(2)}, u32[]{:S(2)}) collective-permute-start(bf16[4,32,128]{2,1,0:T(8,128)(2,1)} %refs_3_.2), channel_id=1, source_target_pairs={{0,4},{4,0},{8,12},{12,8},{1,5},{5,1},{9,13},{13,9},{2,6},{6,2},{1... | collective-permute-start | bytes 98312 | tf_op jit(solution)/shard_map/ppermute | solution.py:96
  4.6 5.3 %collective-permute-start.2 = (bf16[4,32,128]{2,1,0:T(8,128)(2,1)}, bf16[4,32,128]{2,1,0:T(8,128)(2,1)S(1)}, u32[]{:S(2)}, u32[]{:S(2)}) collective-permute-start(bf16[4,32,128]{2,1,0:T(8,128)(2,1)} %refs_3_.2), channel_id=1, source_target_pairs={{0,8},{4,12},{8,0},{12,4},{1,9},{5,13},{9,1},{13,5},{2,10},{6,14},... | collective-permute-start | bytes 98312 | tf_op jit(solution)/shard_map/ppermute | solution.py:96
  7.2 5.9 %collective-permute-start.4 = (bf16[4,32,128]{2,1,0:T(8,128)(2,1)}, bf16[4,32,128]{2,1,0:T(8,128)(2,1)S(1)}, u32[]{:S(2)}, u32[]{:S(2)}) collective-permute-start(bf16[4,32,128]{2,1,0:T(8,128)(2,1)} %refs_3_.2), channel_id=1, source_target_pairs={{0,12},{4,8},{8,4},{12,0},{1,13},{5,9},{9,5},{13,1},{2,14},{6,10},... | collective-permute-start | bytes 98312 | tf_op jit(solution)/shard_map/ppermute | solution.py:96
  7.4 7.2 %collective-permute-start.6 = (bf16[4,32,128]{2,1,0:T(8,128)(2,1)}, bf16[4,32,128]{2,1,0:T(8,128)(2,1)S(1)}, u32[]{:S(2)}, u32[]{:S(2)}) collective-permute-start(bf16[4,32,128]{2,1,0:T(8,128)(2,1)} %refs_3_.2), channel_id=1, source_target_pairs={{0,1},{1,0},{2,3},{3,2},{4,5},{5,4},{6,7},{7,6},{8,9},{9,8},{10,11... | collective-permute-start | bytes 98312 | tf_op jit(solution)/shard_map/ppermute | solution.py:96
  7.4 8.3 %collective-permute-start.1 = (bf16[4,32,128]{2,1,0:T(8,128)(2,1)S(1)}, bf16[4,32,128]{2,1,0:T(8,128)(2,1)S(1)}, u32[]{:S(2)}, u32[]{:S(2)}) collective-permute-start(bf16[4,32,128]{2,1,0:T(8,128)(2,1)S(1)} %collective-permute-done.refs_1_), channel_id=1, source_target_pairs={{0,1},{1,0},{2,3},{3,2},{4,5},{5,4},{6,7},{7,6},{8,9},{9,8},{10,11... | collective-permute-start | bytes 98312 | tf_op jit(solution)/shard_map/ppermute | solution.py:96
  9.9 5.8 %collective-permute-start.3 = (bf16[4,32,128]{2,1,0:T(8,128)(2,1)S(1)}, bf16[4,32,128]{2,1,0:T(8,128)(2,1)S(1)}, u32[]{:S(2)}, u32[]{:S(2)}) collective-permute-start(bf16[4,32,128]{2,1,0:T(8,128)(2,1)S(1)} %collective-permute-done.2.refs_2_), channel_id=1, source_target_pairs={{0,1},{1,0},{2,3},{3,2},{4,5},{5,4},{6,7},{7,6},{8,9},{9,8},{10,11... | collective-permute-start | bytes 98312 | tf_op jit(solution)/shard_map/ppermute | solution.py:96
  13.1 2.6 %collective-permute-start.5 = (bf16[4,32,128]{2,1,0:T(8,128)(2,1)S(1)}, bf16[4,32,128]{2,1,0:T(8,128)(2,1)S(1)}, u32[]{:S(2)}, u32[]{:S(2)}) collective-permute-start(bf16[4,32,128]{2,1,0:T(8,128)(2,1)S(1)} %collective-permute-done.4.refs_3_), channel_id=1, source_target_pairs={{0,1},{1,0},{2,3},{3,2},{4,5},{5,4},{6,7},{7,6},{8,9},{9,8},{10,11... | collective-permute-start | bytes 98312 | tf_op jit(solution)/shard_map/ppermute | solution.py:96

commit v3 on v0

--- a/solution.py
+++ b/solution.py
@@ -1,9 +1,17 @@
+import functools
+
 import jax
 import jax.numpy as jnp
 from jax import lax
+from jax.experimental import pallas as pl
+from jax.experimental.pallas import tpu as pltpu
 from jax.sharding import PartitionSpec as P
 
+
 epsilon = 1e-05
+
+
+GATHER_LIMIT = 1 << 20
 
 
 def normalize(values, reduce_axis):
@@ -83,7 +91,400 @@
     return finish(triangle.astype(jnp.bfloat16), normed, layer_one, 1)
 
 
+def swap(value, axis, step):
+    count = lax.axis_size(axis)
+    return lax.ppermute(value, axis, [(i, i ^ step) for i in range(count)])
+
+
+def mm(a, b):
+    return jnp.dot(a, b, preferred_element_type=jnp.float32)
+
+
+def mmt(a, b):
+    return lax.dot_general(a, b, (((1,), (1,)), ((), ())), preferred_element_type=jnp.float32)
+
+
+def constants(c):
+    diagonal = lax.broadcasted_iota(jnp.int32, (c, c), 0) == lax.broadcasted_iota(jnp.int32, (c, c), 1)
+    return jnp.where(diagonal, 1.0 - 1.0 / c, -1.0 / c).astype(jnp.bfloat16)
+
+
+def exact(a, b):
+    total = 0.0
+    for _ in range(3):
+        piece = a.astype(jnp.bfloat16)
+        total = total + mm(piece, b)
+        a = a - piece.astype(jnp.float32)
+    return total
+
+
+def layer_norm(values, gain, bias, centring):
+    centred = mm(values, centring)
+    spread = jnp.mean(centred * centred, axis=1, keepdims=True)
+    return (centred * lax.rsqrt(spread + epsilon) * gain + bias).astype(jnp.bfloat16)
+
+
+def gated(half_gate, half_value):
+    return half_value * jnp.tanh(half_gate) + half_value
+
+
+class Place:
+    def __init__(self, counts, length, c):
+        self.rows_count, self.chan_count, self.sub_count, self.size = counts
+        self.length, self.c = length, c
+        self.row = lax.axis_index("rows")
+        self.chan = lax.axis_index("chan")
+        self.sub = lax.axis_index("sub")
+        self.chip = self.size * self.sub_count
+        self.quarter = length // self.chan_count
+        self.area = self.size * length
+        self.centring = constants(c)
+        hops = range(1, self.rows_count)
+        self.early = [(0, 0), *[(rs, 0) for rs in hops], (0, 1)]
+        self.late = [(rs, 1) for rs in hops]
+
+    def at(self, rs, ss):
+        return ((self.row ^ rs) * self.sub_count + (self.sub ^ ss)) * self.size
+
+    def chips(self):
+        return [(self.chan * (self.quarter // self.chip) + i) ^ self.row for i in range(self.quarter // self.chip)]
+
+    def slots(self):
+        return [[self.at(0, 0)], [self.at(rs, 0) for rs in self.chips()], [self.at(rs, 1) for rs in self.chips()]]
+
+    def norm(self, x, gain_ref, bias_ref, layer):
+        return layer_norm(x, gain_ref[layer:layer + 1], bias_ref[layer:layer + 1], self.centring)
+
+    def enter(self, blocks, gain_ref, bias_ref, gw_ref, gate_ref, x_ref):
+        x = jnp.concatenate([b.reshape(self.area, self.c) for b in blocks], 0)
+        normed = self.norm(x, gain_ref, bias_ref, 0)
+        gate_ref[...] = jnp.tanh(mm(normed, gw_ref[0])).reshape(gate_ref.shape)
+        x_ref[...] = x.astype(jnp.float32).reshape(x_ref.shape)
+        return normed
+
+    def edges(self, normed, w_ref, q, row_masks, column_mask):
+        _, _, h, c = w_ref.shape
+        p = mmt(normed, w_ref[0, q:q + 2].reshape(2 * h, c))
+        shape = (normed.shape[0] // self.length, self.length, h)
+        mask = row_masks[:, None, :] * column_mask[None]
+        return gated(p[:, :h].reshape(shape), p[:, h:].reshape(shape) * mask)
+
+    def turned(self, right):
+        tile = right if right.shape[0] == self.chip else jnp.concatenate([right, right], 0)
+        return jnp.swapaxes(tile, 0, 1)
+
+    def triangle(self, left_ref, first, count, turned, tri_refs):
+        h = left_ref.shape[2]
+        low = lax.broadcasted_iota(jnp.int32, (self.chip, h), 0) < self.size
+        acc = {}
+        for m in range(self.length):
+            ls = [left_ref[first + i, m:m + 1, :] for i in range(count)]
+            for t, ref in turned.items():
+                r = ref[m]
+                for i in range(0, count, 2 if t == 0 else 1):
+                    l = jnp.where(low, ls[i], ls[i + 1]) if t == 0 else ls[i]
+                    acc[i, t] = acc[i, t] + l * r if m else l * r
+        for (i, t), value in acc.items():
+            ref, offset = tri_refs[t]
+            ref[offset + ((first + i) // 2 if t == 0 else first + i)] = value
+
+    def tiles(self, read, rows, slot):
+        if slot == 0:
+            parts = [read(pl.ds(i, rows // 2, stride=2), self.slots()[0][0]) for i in range(2)]
+        else:
+            parts = [read(pl.ds(0, rows), o) for o in self.slots()[slot]]
+        tiles = jnp.concatenate(parts, 1)
+        return tiles.reshape(tiles.shape[0] * tiles.shape[1], tiles.shape[2])
+
+    def columns(self, refs):
+        def one(ref, slot):
+            return self.tiles(lambda rows, o: ref[rows, pl.ds(o, self.size), :], ref.shape[0], slot)
+
+        return jnp.concatenate([one(ref, slot) for slot in range(3) for ref in refs], 0)
+
+    def masks(self, mask_ref, row_mask_ref, slot):
+        return self.tiles(
+            lambda rows, o: row_mask_ref[rows][:, None, :] * mask_ref[pl.ds(o, self.size)][None], self.length, slot
+        )
+
+    def column_masks(self, mask_ref, slots):
+        return jnp.concatenate([mask_ref[pl.ds(o, self.size)] for t in slots for o in self.slots()[t]], 0)
+
+
+def keep(place, step, ref, w_ref):
+    part = ref.shape[2]
+    at = pl.multiple_of((place.chan ^ step) * part, part)
+    w_ref[:, :, pl.ds(at, part), :] = ref[...] * jnp.bfloat16(0.5)
+
+
+def early_kernel(counts, *refs):
+    present_ref, ig_ref, ib_ref = refs[:3]
+    sources = refs[3:9]
+    gate_ref, x_ref, w_ref, mask_ref, row_mask_ref, gw_ref, fold_ref, shift_ref, normed_ref = refs[9:18]
+    raw, sems = refs[18:24], refs[24]
+    copies = [pltpu.make_async_copy(a, b, sems.at[i]) for i, (a, b) in enumerate(zip(sources, raw))]
+    for copy in copies:
+        copy.start()
+    length, h = mask_ref.shape
+    place = Place(counts, length, x_ref.shape[2])
+    half = jnp.bfloat16(0.5)
+    across = present_ref[...].astype(jnp.float32)
+    square = (length, length)
+    diagonal = lax.broadcasted_iota(jnp.int32, square, 0) == lax.broadcasted_iota(jnp.int32, square, 1)
+    mask_ref[...] = mm(jnp.where(diagonal, across, 0.0).astype(jnp.bfloat16), jnp.ones((length, h), jnp.bfloat16))
+    for i, where in enumerate(place.early + place.late):
+        row_mask_ref[i * place.size:(i + 1) * place.size] = mask_ref[pl.ds(place.at(*where), place.size)]
+    for copy in copies:
+        copy.wait()
+    pair_ref, projections_ref, gate_weight_ref, ow_ref, og_ref, ob_ref = raw
+    gw_ref[...] = gate_weight_ref[...] * half
+    keep(place, 0, projections_ref, w_ref)
+    normed_ref[...] = place.enter([pair_ref[...]], ig_ref, ib_ref, gw_ref, gate_ref, x_ref)
+    for layer in range(2):
+        out = ow_ref[layer] * half
+        folded = exact(place.centring.astype(jnp.float32) * og_ref[layer:layer + 1], out)
+        high = folded.astype(jnp.bfloat16)
+        fold_ref[layer, :h, :h] = place.centring
+        fold_ref[layer, :h, h:] = high
+        fold_ref[layer, h:, :h] = jnp.zeros((h, h), jnp.bfloat16)
+        fold_ref[layer, h:, h:] = (folded - high.astype(jnp.float32)).astype(jnp.bfloat16)
+        shift_ref[layer] = exact(jnp.broadcast_to(ob_ref[layer:layer + 1], (8, h)), out)
+
+
+def arrived_kernel(counts, *refs):
+    n = counts[0]
+    blocks = refs[:n]
+    ig_ref, ib_ref, gw_ref, own_ref, gate_ref, x_ref, normed_ref = refs[n:]
+    place = Place(counts, x_ref.shape[1], x_ref.shape[2])
+    normed_ref[0] = own_ref[...]
+    normed = place.enter([b[...] for b in blocks], ig_ref, ib_ref, gw_ref, gate_ref, x_ref)
+    normed_ref[1:] = normed.reshape(n, place.area, place.c)
+
+
+def first_kernel(counts, ahead, *refs):
+    n = counts[1] - 1
+    weights = refs[:n]
+    normed_ref, mask_ref, row_mask_ref, _, left_ref, turned_ref, tri_ref, w_ref = refs[n:]
+    place = Place(counts, mask_ref.shape[0], normed_ref.shape[2])
+    for i, ref in enumerate(weights):
+        keep(place, i + 1, ref, w_ref)
+    rows = left_ref.shape[0]
+    mask = mask_ref[...]
+    size = place.size
+    wanted = jnp.concatenate([normed_ref[0], *[normed_ref[rs] for rs in place.chips()]], 0)
+    right = place.edges(wanted, w_ref, 2, place.column_masks(mask_ref, (0, 1)), mask)
+    turned_ref[0] = place.turned(right[:size])
+    turned_ref[1] = place.turned(right[size:])
+    every = normed_ref[...].reshape(-1, place.c)
+    left_ref[...] = place.edges(every, w_ref, 0, row_mask_ref[:rows], mask)
+    for i in range(0, ahead, size):
+        place.triangle(
+            left_ref, i, size, {0: turned_ref.at[0], 1: turned_ref.at[1]}, {0: (tri_ref, 0), 1: (tri_ref, ahead // 2)}
+        )
+
+
+def last_kernel(counts, ahead, *refs):
+    n = counts[0] - 1
+    blocks = refs[:n]
+    (ig_ref, ib_ref, left_ref, turned_ref, tri_ref, gate0_ref, x0_ref, gate1_ref, x1_ref, normed_ref, w_ref, mask_ref,
+     row_mask_ref, gw_ref, fold_ref, shift_ref, out_ref,
+     gate2_ref, x2_ref, others_ref, late_ref, turned2_ref, tri0_ref, tri1_ref, tri2_ref, z_ref, l1_ref, r1_ref) = refs[n:]
+    length, h = mask_ref.shape
+    c = x0_ref.shape[2]
+    place = Place(counts, length, c)
+    size, chip, quarter = place.size, place.chip, place.quarter
+    rows = left_ref.shape[0]
+    mask = mask_ref[...]
+    early_turned = {0: turned_ref.at[0], 1: turned_ref.at[1]}
+    for i in range(ahead, rows, size):
+        place.triangle(left_ref, i, size, early_turned, {0: (tri0_ref, -ahead // 2), 1: (tri1_ref, -ahead)})
+    normed = place.enter([b[...] for b in blocks], ig_ref, ib_ref, gw_ref, gate2_ref, x2_ref)
+    others_ref[0] = normed_ref[counts[0]]
+    others_ref[1:] = normed.reshape(n, place.area, c)
+    wanted = jnp.concatenate([others_ref[rs] for rs in place.chips()], 0)
+    turned2_ref[...] = place.turned(place.edges(wanted, w_ref, 2, place.column_masks(mask_ref, (2,)), mask))
+    late_ref[...] = place.edges(normed, w_ref, 0, row_mask_ref[rows:], mask)
+    for i in range(0, rows, 2 * size):
+        place.triangle(left_ref, i, min(2 * size, rows - i), {2: turned2_ref}, {2: (tri2_ref, 0)})
+    late = late_ref.shape[0]
+    for i in range(0, late, size):
+        place.triangle(
+            late_ref, i, size, {**early_turned, 2: turned2_ref},
+            {0: (tri0_ref, (rows - ahead) // 2), 1: (tri1_ref, rows - ahead), 2: (tri2_ref, rows)},
+        )
+
+    def finish(tri, half_gate, residual, layer):
+        both = tri.astype(jnp.bfloat16)
+        both = mm(jnp.concatenate([both, both], 1), fold_ref[layer])
+        centred = both[:, :h]
+        spread = jnp.mean(centred * centred, axis=1, keepdims=True)
+        update = both[:, h:] * lax.rsqrt(spread + epsilon) + shift_ref[layer, 0:1]
+        return (residual + (update * half_gate + update)).astype(jnp.bfloat16)
+
+    half_gate = place.columns((gate0_ref, gate1_ref, gate2_ref))
+    residual = place.columns((x0_ref, x1_ref, x2_ref))
+    tri = jnp.concatenate([tri_ref[:ahead // 2], tri0_ref[...], tri_ref[ahead // 2:], tri1_ref[...], tri2_ref[...]], 0)
+    z = finish(tri.reshape(residual.shape[0], h), half_gate, residual, 0)
+    area = length * size
+    z_ref[...] = z[area:].astype(jnp.float32).reshape(2, length, chip, c)
+
+    normed = place.norm(z, ig_ref, ib_ref, 1)
+    p = mmt(normed[:area], w_ref[1, 0:2].reshape(2 * h, c))
+    l1_ref[...] = gated(p[:, :h], p[:, h:] * place.masks(mask_ref, row_mask_ref, 0))
+    p = mmt(normed[area:], w_ref[1, 2:4].reshape(2 * h, c))
+    area = length * chip
+    for t in (1, 2):
+        at = slice((t - 1) * area, t * area)
+        r1_ref[t - 1] = gated(p[at, :h], p[at, h:] * place.masks(mask_ref, row_mask_ref, t)).reshape(length, chip, h)
+    mine = z_ref[:, :size].reshape(2 * size * chip, c)
+    half_gate = jnp.tanh(mm(place.norm(mine.astype(jnp.bfloat16), ig_ref, ib_ref, 1), gw_ref[1]))
+
+    acc = [jnp.zeros((chip, h), jnp.float32) for _ in range(2 * size)]
+    for k in range(length):
+        rs = [r1_ref[t, k] for t in range(2)]
+        ls = [l1_ref[k * size + i:k * size + i + 1, :] for i in range(size)]
+        acc = [acc[t * size + i] + ls[i] * rs[t] for t in range(2) for i in range(size)]
+    z = finish(jnp.concatenate(acc, 0), half_gate, mine, 1).astype(jnp.float32).reshape(2, size, chip, c)
+    even = jnp.where(place.sub == 0, z[0], z[1])
+    odd = jnp.where(place.sub == 0, z[1], z[0])
+    parts = [v[:, i * size:(i + 1) * size] for i in range(quarter // chip) for v in (even, odd)]
+    out_ref[...] = jnp.concatenate(parts, 1).astype(jnp.bfloat16)
+
+
+def in_vmem(value):
+    return pltpu.with_memory_space_constraint(value, pltpu.VMEM)
+
+
+def in_hbm(value):
+    return pltpu.with_memory_space_constraint(value, pltpu.HBM)
+
+
+VMEM = pl.BlockSpec(memory_space=pltpu.VMEM)
+HBM = pl.BlockSpec(memory_space=pltpu.HBM)
+
+AHEAD = 8
+
+
+def gathered(
+    pair, residue_mask, in_gain, in_bias, projections, gate_weight, out_gain, out_bias, out_weight
+):
+    rows_count, chan_count, sub_count = (lax.axis_size(a) for a in ("rows", "chan", "sub"))
+    size, length, c = pair.shape
+    h = out_weight.shape[1]
+    chip, area = size * sub_count, size * length
+    counts = (rows_count, chan_count, sub_count, size)
+    turned = jnp.swapaxes(projections, 2, 3)
+    hops = tuple(range(1, rows_count))
+    far, near = {}, {}
+    for rs in hops:
+        far[rs] = swap(pair, "rows", rs)
+    near[0] = swap(pair, "sub", 1)
+    weights = [swap(turned, "chan", i) for i in range(1, chan_count)]
+    for rs in hops:
+        near[rs] = swap(far[rs], "sub", 1)
+
+    def f32(*shape):
+        return pltpu.VMEM(shape, jnp.float32)
+
+    def bf16(*shape):
+        return pltpu.VMEM(shape, jnp.bfloat16)
+
+    def call(kernel, near, far, out_shape, scratch=(), aliases={}, rows=0, mib=8):
+        return pl.pallas_call(
+            kernel,
+            out_shape=out_shape,
+            in_specs=[VMEM] * len(near) + [HBM] * len(far),
+            out_specs=jax.tree.map(lambda _: VMEM, out_shape),
+            scratch_shapes=[
+                *scratch,
+                *[pltpu.VMEM(o.shape, o.dtype) for o in far],
+                *([pltpu.SemaphoreType.DMA((len(far),))] if far else []),
+            ],
+            input_output_aliases=aliases,
+            compiler_params=pltpu.CompilerParams(vmem_limit_bytes=mib << 20),
+            cost_estimate=pl.CostEstimate(flops=rows * c * c * 16, bytes_accessed=0, transcendentals=0),
+        )(*[in_vmem(o) for o in near], *[in_hbm(o) for o in far])
+
+    gate0, x0, w, mask, row_mask, gw, fold, shift, own = call(
+        functools.partial(early_kernel, counts),
+        [residue_mask[None], in_gain, in_bias],
+        [pair, turned, gate_weight, out_weight, out_gain, out_bias],
+        [
+            f32(size, length, c),
+            f32(size, length, c),
+            bf16(2, 4, h, c),
+            f32(length, h),
+            f32(length, h),
+            bf16(2, c, c),
+            bf16(2, 2 * h, h + c),
+            f32(2, 8, c),
+            bf16(area, c),
+        ],
+        rows=length * length,
+    )
+    gate1, x1, normed = call(
+        functools.partial(arrived_kernel, counts),
+        [*[far[rs] for rs in hops], near[0], in_gain, in_bias, gw, own],
+        [],
+        [
+            f32(rows_count * size, length, c),
+            f32(rows_count * size, length, c),
+            bf16(rows_count + 1, area, c),
+        ],
+        rows=length * length,
+    )
+    early = (rows_count + 1) * size
+    late = length - early
+    operands = [*weights, normed, mask, row_mask, w]
+    left, right, tri, w = call(
+        functools.partial(first_kernel, counts, AHEAD),
+        operands,
+        [],
+        [f32(early, length, h), f32(2, length, chip, h), f32(AHEAD // 2 + AHEAD, chip, h), bf16(2, 4, h, c)],
+        aliases={len(operands) - 1: 3},
+        rows=length * length,
+    )
+    operands = [
+        *[near[rs] for rs in hops], in_gain, in_bias, left, right, tri, gate0, x0, gate1, x1, normed, w, mask, row_mask,
+        gw, fold, shift,
+    ]
+    return call(
+        functools.partial(last_kernel, counts, AHEAD),
+        operands,
+        [],
+        jax.ShapeDtypeStruct((size, length // chan_count, c), jnp.bfloat16),
+        scratch=[
+            f32(late, length, c),
+            f32(late, length, c),
+            bf16(rows_count, area, c),
+            f32(late, length, h),
+            f32(length, chip, h),
+            f32((length - AHEAD) // 2, chip, h),
+            f32(length - AHEAD, chip, h),
+            f32(length, chip, h),
+            f32(2, length, chip, c),
+            f32(length * size, h),
+            f32(2, length, chip, h),
+        ],
+        rows=1,
+        mib=16,
+    )
+
+
 def solution(mesh):
+    def body(pair, *rest):
+        size, length, c = pair.shape
+        small = 2 * length * length * c <= GATHER_LIMIT
+        fits = (
+            mesh.shape["sub"] == 2
+            and mesh.shape["rows"] & (mesh.shape["rows"] - 1) == 0
+            and size * 2 == 8
+            and length == 16 * mesh.shape["chan"]
+        )
+        if not (small and fits):
+            return shards(pair, *rest)
+        return gathered(pair, *rest)
+
     placed = (
         P(("crops", "rows", "sub"), None, None),
         P("crops"),
@@ -95,10 +496,13 @@
         P(),
         P(),
     )
-    return jax.shard_map(
-        shards,
+    step = jax.shard_map(
+        body,
         mesh=mesh,
         in_specs=placed,
         out_specs=P(("crops", "rows", "sub"), "chan", None),
         check_vma=False,
     )
+    if 8 * mesh.shape["rows"] != 16 * mesh.shape["chan"]:
+        return step
+    return step

time: 74.4 us -> 15.8 us (0.21)
  blocking collectives: 35 us -> 0 us
  waiting for transfers between devices: 11.4 us -> 2.52 us
  local copies, waits for them, and re-layouts: 7.84 us -> 0.01 us
  starting transfers between devices: 14.5 us -> 8.15 us
  Pallas kernels: 0 us -> 4.94 us
  other arithmetic: 2.48 us -> 0 us
  matrix products: 2.32 us -> 0 us
    all_gather x3 -> x0, blocking collectives: 35 us -> none  [the longest x1 15.9 us: shards(): lax.all_gather(right_edges, ('rows', 'sub'), axis=1, tiled=True)]
    all_to_all x4 -> x0, starting transfers between devices: 14.5 us -> none  [the longest x2 6.47 us: finish(): lax.all_to_all(triangle, 'chan', split_axis=2, concat_axis=0, tiled=True)]
    all_to_all x4 -> x0, waiting for transfers between devices: 11.4 us -> none  [the longest x2 6.63 us: finish(): lax.all_to_all(triangle, 'chan', split_axis=2, concat_axis=0, tiled=True)]
    ppermute x0 -> x8, starting transfers between devices: none -> 8.15 us  [swap(): return lax.ppermute(value, axis, [(i, i ^ step) for i in range(count)])]
    unnamed x26 -> x6, local copies, waits for them, and re-layouts: 5.09 us -> 0.01 us
    pallas_call x0 -> x4, Pallas kernels: none -> 4.94 us  [call(): pl.pallas_call(kernel, out_shape=out_shape, in_specs=[VMEM] * len(near) +...]
    ppermute x0 -> x8, waiting for transfers between devices: none -> 2.52 us  [swap(): return lax.ppermute(value, axis, [(i, i ^ step) for i in range(count)])]
    dot_general x8 -> x0, matrix products: 2.32 us -> none  [the longest x2 0.87 us: finish(): jnp.einsum('hij,hc->ijc', scaled, out_weight[layer_index], preferred_elem...]
  transfers between devices with their start and end apart: 4 -> 8, of which waited for: 3 -> 2; matrix products, arithmetic and copies ran while one was open for 3% -> 0% of each run, Pallas kernels for 0% -> 15%
where the time goes in v3:
time: 15.8 us; the launch traced here: 15.7 us
  starting transfers between devices  8.15 us (52%)
  Pallas kernels  4.94 us (31%)
  waiting for transfers between devices  2.52 us (16%)
    ppermute x8, starting transfers between devices, swap(): return lax.ppermute(value, axis, [(i, i ^ step) for i in range(count)])  8.15 us
    pallas_call x4, Pallas kernels, call(): pl.pallas_call(kernel, out_shape=out_shape, in_specs=[VMEM] * len(near) +...  4.94 us
    ppermute x8, waiting for transfers between devices, swap(): return lax.ppermute(value, axis, [(i, i ^ step) for i in range(count)])  2.52 us
  transfers between devices with their start and end apart: 8, of which 2 were waited for; matrix products, arithmetic and copies ran while one was open for 0% of the time, Pallas kernels for 15%

profile of v3, /device:TPU:0, one launch (start us, length us, event | category | flops | bytes accessed | tf_op | source)
XLA Modules:
  0.0 15.7 jit_solution(14343209310869628338)
XLA Ops:
  0.0 0.0 copy-start.1
  0.0 0.0 copy-start
  0.0 0.0 copy-start.2
  0.0 3.0 %collective-permute-start.6 = (bf16[2,4,64,128]{3,2,1,0:T(8,128)(2,1)}, bf16[2,4,64,128]{3,2,1,0:T(8,128)(2,1)S(1)}, u32[]{:S(2)}, u32[]{:S(2)}) collective-permute-start(bf16[2,4,64,128]{3,2,1,0:T(8,128)(2,1)} %bitcast.3), channel_id=1, source_target_pairs={{0,2},{2,0},{1,3},{3,1},{4,6},{6,4},{5,7},{7,5},{8,10},{10,8},{9,1... | collective-permute-start | bytes 393224 | tf_op jit(solution)/shard_map/ppermute | solution.py:96
  3.0 3.6 %collective-permute-start.4 = (bf16[4,32,128]{2,1,0:T(8,128)(2,1)}, bf16[4,32,128]{2,1,0:T(8,128)(2,1)S(1)}, u32[]{:S(2)}, u32[]{:S(2)}) collective-permute-start(bf16[4,32,128]{2,1,0:T(8,128)(2,1)} %refs_3_.2), channel_id=1, source_target_pairs={{0,12},{4,8},{8,4},{12,0},{1,13},{5,9},{9,5},{13,1},{2,14},{6,10},... | collective-permute-start | bytes 98312 | tf_op jit(solution)/shard_map/ppermute | solution.py:96
  6.6 0.0 collective-permute-start.2
  6.6 0.8 %collective-permute-start = (bf16[4,32,128]{2,1,0:T(8,128)(2,1)}, bf16[4,32,128]{2,1,0:T(8,128)(2,1)S(1)}, u32[]{:S(2)}, u32[]{:S(2)}) collective-permute-start(bf16[4,32,128]{2,1,0:T(8,128)(2,1)} %refs_3_.2), channel_id=1, source_target_pairs={{0,4},{4,0},{8,12},{12,8},{1,5},{5,1},{9,13},{13,9},{2,6},{6,2},{1... | collective-permute-start | bytes 98312 | tf_op jit(solution)/shard_map/ppermute | solution.py:96
  7.4 0.0 collective-permute-start.7
  7.4 0.0 copy-done.1
  7.4 0.0 copy-done
  7.4 0.0 copy-done.2
  7.5 1.5 %shard_map.91 = (f32[4,32,128]{2,1,0:T(8,128)S(1)}, f32[4,32,128]{2,1,0:T(8,128)S(1)}, bf16[2,4,128,128]{3,2,1,0:T(8,128)(2,1)S(1)}, f32[32,128]{1,0:T(8,128)S(1...) custom-call(s32[1,32]{1,0:T(1,128)S(1)} %bitcast.2, ...), custom_call_target="tpu_custom_call" | custom-call | flops 268435456 | tf_op jit(solution)/shard_map/pallas_call | solution.py:393
  9.0 0.4 %collective-permute-done.4.refs_2_ = bf16[4,32,128]{2,1,0:T(8,128)(2,1)S(1)} collective-permute-done((bf16[4,32,128]{2,1,0:T(8,128)(2,1)}, bf16[4,32,128]{2,1,0:T(8,128)(2,1)S(1)}, u32[]{:S(2)}, u32[]{:S(2)}) %collective-permute-start.4) | collective-permute-done | bytes 32800 | tf_op jit(solution)/shard_map/ppermute | solution.py:96
  9.3 0.2 %collective-permute-start.5 = (bf16[4,32,128]{2,1,0:T(8,128)(2,1)S(1)}, bf16[4,32,128]{2,1,0:T(8,128)(2,1)S(1)}, u32[]{:S(2)}, u32[]{:S(2)}) collective-permute-start(bf16[4,32,128]{2,1,0:T(8,128)(2,1)S(1)} %collective-permute-done.4.refs_2_), channel_id=1, source_target_pairs={{0,1},{1,0},{2,3},{3,2},{4,5},{5,4},{6,7},{7,6},{8,9},{9,8},{10,11... | collective-permute-start | bytes 98312 | tf_op jit(solution)/shard_map/ppermute | solution.py:96
  9.5 2.1 %collective-permute-done.2.refs_1_ = bf16[4,32,128]{2,1,0:T(8,128)(2,1)S(1)} collective-permute-done((bf16[4,32,128]{2,1,0:T(8,128)(2,1)}, bf16[4,32,128]{2,1,0:T(8,128)(2,1)S(1)}, u32[]{:S(2)}, u32[]{:S(2)}) %collective-permute-start.2) | collective-permute-done | bytes 32800 | tf_op jit(solution)/shard_map/ppermute | solution.py:96
  11.7 0.0 collective-permute-start.3
  11.7 0.0 collective-permute-done.refs_0_
  11.7 0.5 %collective-permute-start.1 = (bf16[4,32,128]{2,1,0:T(8,128)(2,1)S(1)}, bf16[4,32,128]{2,1,0:T(8,128)(2,1)S(1)}, u32[]{:S(2)}, u32[]{:S(2)}) collective-permute-start(bf16[4,32,128]{2,1,0:T(8,128)(2,1)S(1)} %collective-permute-done.refs_0_), channel_id=1, source_target_pairs={{0,1},{1,0},{2,3},{3,2},{4,5},{5,4},{6,7},{7,6},{8,9},{9,8},{10,11... | collective-permute-start | bytes 98312 | tf_op jit(solution)/shard_map/ppermute | solution.py:96
  12.2 0.0 collective-permute-done.7.refs_3_
  12.2 0.4 %shard_map.92 = (f32[16,32,128]{2,1,0:T(8,128)S(1)}, f32[16,32,128]{2,1,0:T(8,128)S(1)}, bf16[5,128,128]{2,1,0:T(8,128)(2,1)S(1)}) custom-call(bf16[4,32,128]{2,1,0:T(8,128)(2,1)S(1)} %collective-permute-done.refs_0_, bf16[4,32,128]{2,1,0:T(8,128)(2,1)S(1)} %collective-permute-done.2.refs_1_, bf16[4,32,128]{2,1,0:T(8,128)(2,1)S(1)} %collective-permute-done.4.refs_2_, ...), custom_call_target="tpu_custom_call" | custom-call | flops 268435456 | tf_op jit(solution)/shard_map/pallas_call | solution.py:393
  12.6 0.0 collective-permute-done.6.refs_0_
  12.6 0.5 %shard_map.93 = (f32[20,32,128]{2,1,0:T(8,128)S(1)}, f32[2,32,8,128]{3,2,1,0:T(8,128)S(1)}, f32[12,8,128]{2,1,0:T(8,128)S(1)}, bf16[2,4,128,128]{3,2,1,0:T(8,128)(2,1)S(1)}) custom-call(bf16[2,4,64,128]{3,2,1,0:T(8,128)(2,1)S(1)} %collective-permute-done.6.refs_0_, ...), custom_call_target="tpu_custom_call", output_to_operand_aliasing={{3}: (4, {})} | custom-call | flops 268435456 | tf_op jit(solution)/shard_map/pallas_call | solution.py:393
  13.1 0.0 collective-permute-done.5.refs_2_
  13.1 0.0 collective-permute-done.3.refs_1_
  13.1 0.0 collective-permute-done.1.refs_0_
  13.1 2.5 %shard_map.94 = bf16[4,16,128]{2,1,0:T(8,128)(2,1)} custom-call(bf16[4,32,128]{2,1,0:T(8,128)(2,1)S(1)} %collective-permute-done.1.refs_0_, bf16[4,32,128]{2,1,0:T(8,128)(2,1)S(1)} %collective-permute-done.3.refs_1_, bf16[4,32,128]{2,1,0:T(8,128)(2,1)S(1)} %collective-permute-done.5.refs_2_, f32[2,128]{1,0:T(2,128)S(1)} %copy-done, f32[2,128]{1,0:T(2,128)S(1)} %copy-done.1, ...), custom_call_target="tpu_custom_call" | custom-call | flops 262144 | tf_op jit(solution)/shard_map/pallas_call | solution.py:393
Async XLA Ops:
  0.0 7.4 %copy-start.1 = (f32[2,128]{1,0:T(2,128)S(1)}, f32[2,128]{1,0:T(2,128)}, u32[]{:S(2)}) copy-start(f32[2,128]{1,0:T(2,128)} %refs_4_.3) | copy-start | bytes 3076
  0.0 7.4 %copy-start = (f32[2,128]{1,0:T(2,128)S(1)}, f32[2,128]{1,0:T(2,128)}, u32[]{:S(2)}) copy-start(f32[2,128]{1,0:T(2,128)} %refs_3_.3) | copy-start | bytes 3076
  0.0 7.4 %copy-start.2 = (s32[32]{0:T(128)S(1)}, s32[32]{0:T(128)}, u32[]{:S(2)}) copy-start(s32[32]{0:T(128)} %param.10) | copy-start | bytes 388
  0.0 12.6 %collective-permute-start.6 = (bf16[2,4,64,128]{3,2,1,0:T(8,128)(2,1)}, bf16[2,4,64,128]{3,2,1,0:T(8,128)(2,1)S(1)}, u32[]{:S(2)}, u32[]{:S(2)}) collective-permute-start(bf16[2,4,64,128]{3,2,1,0:T(8,128)(2,1)} %bitcast.3), channel_id=1, source_target_pairs={{0,2},{2,0},{1,3},{3,1},{4,6},{6,4},{5,7},{7,5},{8,10},{10,8},{9,1... | collective-permute-start | bytes 393224 | tf_op jit(solution)/shard_map/ppermute | solution.py:96
  3.0 6.3 %collective-permute-start.4 = (bf16[4,32,128]{2,1,0:T(8,128)(2,1)}, bf16[4,32,128]{2,1,0:T(8,128)(2,1)S(1)}, u32[]{:S(2)}, u32[]{:S(2)}) collective-permute-start(bf16[4,32,128]{2,1,0:T(8,128)(2,1)} %refs_3_.2), channel_id=1, source_target_pairs={{0,12},{4,8},{8,4},{12,0},{1,13},{5,9},{9,5},{13,1},{2,14},{6,10},... | collective-permute-start | bytes 98312 | tf_op jit(solution)/shard_map/ppermute | solution.py:96
  6.6 5.0 %collective-permute-start.2 = (bf16[4,32,128]{2,1,0:T(8,128)(2,1)}, bf16[4,32,128]{2,1,0:T(8,128)(2,1)S(1)}, u32[]{:S(2)}, u32[]{:S(2)}) collective-permute-start(bf16[4,32,128]{2,1,0:T(8,128)(2,1)} %refs_3_.2), channel_id=1, source_target_pairs={{0,8},{4,12},{8,0},{12,4},{1,9},{5,13},{9,1},{13,5},{2,10},{6,14},... | collective-permute-start | bytes 98312 | tf_op jit(solution)/shard_map/ppermute | solution.py:96
  6.6 5.0 %collective-permute-start = (bf16[4,32,128]{2,1,0:T(8,128)(2,1)}, bf16[4,32,128]{2,1,0:T(8,128)(2,1)S(1)}, u32[]{:S(2)}, u32[]{:S(2)}) collective-permute-start(bf16[4,32,128]{2,1,0:T(8,128)(2,1)} %refs_3_.2), channel_id=1, source_target_pairs={{0,4},{4,0},{8,12},{12,8},{1,5},{5,1},{9,13},{13,9},{2,6},{6,2},{1... | collective-permute-start | bytes 98312 | tf_op jit(solution)/shard_map/ppermute | solution.py:96
  7.4 4.8 %collective-permute-start.7 = (bf16[4,32,128]{2,1,0:T(8,128)(2,1)}, bf16[4,32,128]{2,1,0:T(8,128)(2,1)S(1)}, u32[]{:S(2)}, u32[]{:S(2)}) collective-permute-start(bf16[4,32,128]{2,1,0:T(8,128)(2,1)} %refs_3_.2), channel_id=1, source_target_pairs={{0,1},{1,0},{2,3},{3,2},{4,5},{5,4},{6,7},{7,6},{8,9},{9,8},{10,11... | collective-permute-start | bytes 98312 | tf_op jit(solution)/shard_map/ppermute | solution.py:96
  9.3 3.8 %collective-permute-start.5 = (bf16[4,32,128]{2,1,0:T(8,128)(2,1)S(1)}, bf16[4,32,128]{2,1,0:T(8,128)(2,1)S(1)}, u32[]{:S(2)}, u32[]{:S(2)}) collective-permute-start(bf16[4,32,128]{2,1,0:T(8,128)(2,1)S(1)} %collective-permute-done.4.refs_2_), channel_id=1, source_target_pairs={{0,1},{1,0},{2,3},{3,2},{4,5},{5,4},{6,7},{7,6},{8,9},{9,8},{10,11... | collective-permute-start | bytes 98312 | tf_op jit(solution)/shard_map/ppermute | solution.py:96
  11.7 1.5 %collective-permute-start.3 = (bf16[4,32,128]{2,1,0:T(8,128)(2,1)S(1)}, bf16[4,32,128]{2,1,0:T(8,128)(2,1)S(1)}, u32[]{:S(2)}, u32[]{:S(2)}) collective-permute-start(bf16[4,32,128]{2,1,0:T(8,128)(2,1)S(1)} %collective-permute-done.2.refs_1_), channel_id=1, source_target_pairs={{0,1},{1,0},{2,3},{3,2},{4,5},{5,4},{6,7},{7,6},{8,9},{9,8},{10,11... | collective-permute-start | bytes 98312 | tf_op jit(solution)/shard_map/ppermute | solution.py:96
  11.7 1.5 %collective-permute-start.1 = (bf16[4,32,128]{2,1,0:T(8,128)(2,1)S(1)}, bf16[4,32,128]{2,1,0:T(8,128)(2,1)S(1)}, u32[]{:S(2)}, u32[]{:S(2)}) collective-permute-start(bf16[4,32,128]{2,1,0:T(8,128)(2,1)S(1)} %collective-permute-done.refs_0_), channel_id=1, source_target_pairs={{0,1},{1,0},{2,3},{3,2},{4,5},{5,4},{6,7},{7,6},{8,9},{9,8},{10,11... | collective-permute-start | bytes 98312 | tf_op jit(solution)/shard_map/ppermute | solution.py:96

commit v4 on v3

--- a/solution.py
+++ b/solution.py
@@ -162,11 +162,10 @@
         x_ref[...] = x.astype(jnp.float32).reshape(x_ref.shape)
         return normed
 
-    def edges(self, normed, w_ref, q, row_masks, column_mask):
+    def edges(self, normed, w_ref, q, mask):
         _, _, h, c = w_ref.shape
         p = mmt(normed, w_ref[0, q:q + 2].reshape(2 * h, c))
         shape = (normed.shape[0] // self.length, self.length, h)
-        mask = row_masks[:, None, :] * column_mask[None]
         return gated(p[:, :h].reshape(shape), p[:, h:].reshape(shape) * mask)
 
     def turned(self, right):
@@ -272,11 +271,11 @@
     mask = mask_ref[...]
     size = place.size
     wanted = jnp.concatenate([normed_ref[0], *[normed_ref[rs] for rs in place.chips()]], 0)
-    right = place.edges(wanted, w_ref, 2, place.column_masks(mask_ref, (0, 1)), mask)
+    right = place.edges(wanted, w_ref, 2, place.column_masks(mask_ref, (0, 1))[:, None, :] * mask[None])
     turned_ref[0] = place.turned(right[:size])
     turned_ref[1] = place.turned(right[size:])
     every = normed_ref[...].reshape(-1, place.c)
-    left_ref[...] = place.edges(every, w_ref, 0, row_mask_ref[:rows], mask)
+    left_ref[...] = place.edges(every, w_ref, 0, row_mask_ref[:rows][:, None, :])
     for i in range(0, ahead, size):
         place.triangle(
             left_ref, i, size, {0: turned_ref.at[0], 1: turned_ref.at[1]}, {0: (tri_ref, 0), 1: (tri_ref, ahead // 2)}
@@ -288,7 +287,7 @@
     blocks = refs[:n]
     (ig_ref, ib_ref, left_ref, turned_ref, tri_ref, gate0_ref, x0_ref, gate1_ref, x1_ref, normed_ref, w_ref, mask_ref,
      row_mask_ref, gw_ref, fold_ref, shift_ref, out_ref,
-     gate2_ref, x2_ref, others_ref, late_ref, turned2_ref, tri0_ref, tri1_ref, tri2_ref, z_ref, l1_ref, r1_ref) = refs[n:]
+     gate2_ref, x2_ref, others_ref, late_ref, turned2_ref, tri0_ref, tri1_ref, tri2_ref, l1_ref, r1_ref) = refs[n:]
     length, h = mask_ref.shape
     c = x0_ref.shape[2]
     place = Place(counts, length, c)
@@ -302,8 +301,10 @@
     others_ref[0] = normed_ref[counts[0]]
     others_ref[1:] = normed.reshape(n, place.area, c)
     wanted = jnp.concatenate([others_ref[rs] for rs in place.chips()], 0)
-    turned2_ref[...] = place.turned(place.edges(wanted, w_ref, 2, place.column_masks(mask_ref, (2,)), mask))
-    late_ref[...] = place.edges(normed, w_ref, 0, row_mask_ref[rows:], mask)
+    turned2_ref[...] = place.turned(
+        place.edges(wanted, w_ref, 2, place.column_masks(mask_ref, (2,))[:, None, :] * mask[None])
+    )
+    late_ref[...] = place.edges(normed, w_ref, 0, row_mask_ref[rows:][:, None, :])
     for i in range(0, rows, 2 * size):
         place.triangle(left_ref, i, min(2 * size, rows - i), {2: turned2_ref}, {2: (tri2_ref, 0)})
     late = late_ref.shape[0]
@@ -326,18 +327,21 @@
     tri = jnp.concatenate([tri_ref[:ahead // 2], tri0_ref[...], tri_ref[ahead // 2:], tri1_ref[...], tri2_ref[...]], 0)
     z = finish(tri.reshape(residual.shape[0], h), half_gate, residual, 0)
     area = length * size
-    z_ref[...] = z[area:].astype(jnp.float32).reshape(2, length, chip, c)
 
     normed = place.norm(z, ig_ref, ib_ref, 1)
+    starts = [area + t * length * chip for t in range(2)]
+    mine = jnp.concatenate([z[a:a + size * chip] for a in starts], 0).astype(jnp.float32)
+    mine_normed = jnp.concatenate([normed[a:a + size * chip] for a in starts], 0)
     p = mmt(normed[:area], w_ref[1, 0:2].reshape(2 * h, c))
     l1_ref[...] = gated(p[:, :h], p[:, h:] * place.masks(mask_ref, row_mask_ref, 0))
     p = mmt(normed[area:], w_ref[1, 2:4].reshape(2 * h, c))
     area = length * chip
     for t in (1, 2):
         at = slice((t - 1) * area, t * area)
-        r1_ref[t - 1] = gated(p[at, :h], p[at, h:] * place.masks(mask_ref, row_mask_ref, t)).reshape(length, chip, h)
-    mine = z_ref[:, :size].reshape(2 * size * chip, c)
-    half_gate = jnp.tanh(mm(place.norm(mine.astype(jnp.bfloat16), ig_ref, ib_ref, 1), gw_ref[1]))
+        columns = place.column_masks(mask_ref, (t,))[None]
+        shape = (length, chip, h)
+        r1_ref[t - 1] = gated(p[at, :h].reshape(shape), p[at, h:].reshape(shape) * columns)
+    half_gate = jnp.tanh(mm(mine_normed, gw_ref[1]))
 
     acc = [jnp.zeros((chip, h), jnp.float32) for _ in range(2 * size)]
     for k in range(length):
@@ -362,7 +366,7 @@
 VMEM = pl.BlockSpec(memory_space=pltpu.VMEM)
 HBM = pl.BlockSpec(memory_space=pltpu.HBM)
 
-AHEAD = 8
+AHEAD = 12
 
 
 def gathered(
@@ -462,7 +466,6 @@
             f32((length - AHEAD) // 2, chip, h),
             f32(length - AHEAD, chip, h),
             f32(length, chip, h),
-            f32(2, length, chip, c),
             f32(length * size, h),
             f32(2, length, chip, h),
         ],

time: 15.8 us -> 15.8 us (level)
  transfers between devices with their start and end apart: 8 -> 8, of which waited for: 2 -> 2; matrix products, arithmetic and copies ran while one was open for 0% -> 0% of each run, Pallas kernels for 15% -> 16%
where the time goes in v4:
time: 15.8 us; the launch traced here: 15.7 us
  starting transfers between devices  8.15 us (52%)
  Pallas kernels  4.95 us (31%)
  waiting for transfers between devices  2.52 us (16%)
    ppermute x8, starting transfers between devices, swap(): return lax.ppermute(value, axis, [(i, i ^ step) for i in range(count)])  8.15 us
    pallas_call x4, Pallas kernels, call(): pl.pallas_call(kernel, out_shape=out_shape, in_specs=[VMEM] * len(near) +...  4.95 us
    ppermute x8, waiting for transfers between devices, swap(): return lax.ppermute(value, axis, [(i, i ^ step) for i in range(count)])  2.52 us
  transfers between devices with their start and end apart: 8, of which 2 were waited for; matrix products, arithmetic and copies ran while one was open for 0% of the time, Pallas kernels for 16%

profile of v4, /device:TPU:0, one launch (start us, length us, event | category | flops | bytes accessed | tf_op | source)
XLA Modules:
  0.0 15.7 jit_solution(15292142090560536110)
XLA Ops:
  0.0 0.0 copy-start.1
  0.0 0.0 copy-start
  0.0 0.0 copy-start.2
  0.0 3.0 %collective-permute-start.6 = (bf16[2,4,64,128]{3,2,1,0:T(8,128)(2,1)}, bf16[2,4,64,128]{3,2,1,0:T(8,128)(2,1)S(1)}, u32[]{:S(2)}, u32[]{:S(2)}) collective-permute-start(bf16[2,4,64,128]{3,2,1,0:T(8,128)(2,1)} %bitcast.3), channel_id=1, source_target_pairs={{0,2},{2,0},{1,3},{3,1},{4,6},{6,4},{5,7},{7,5},{8,10},{10,8},{9,1... | collective-permute-start | bytes 393224 | tf_op jit(solution)/shard_map/ppermute | solution.py:96
  3.0 3.6 %collective-permute-start.4 = (bf16[4,32,128]{2,1,0:T(8,128)(2,1)}, bf16[4,32,128]{2,1,0:T(8,128)(2,1)S(1)}, u32[]{:S(2)}, u32[]{:S(2)}) collective-permute-start(bf16[4,32,128]{2,1,0:T(8,128)(2,1)} %refs_3_.2), channel_id=1, source_target_pairs={{0,12},{4,8},{8,4},{12,0},{1,13},{5,9},{9,5},{13,1},{2,14},{6,10},... | collective-permute-start | bytes 98312 | tf_op jit(solution)/shard_map/ppermute | solution.py:96
  6.6 0.0 collective-permute-start.2
  6.6 0.8 %collective-permute-start = (bf16[4,32,128]{2,1,0:T(8,128)(2,1)}, bf16[4,32,128]{2,1,0:T(8,128)(2,1)S(1)}, u32[]{:S(2)}, u32[]{:S(2)}) collective-permute-start(bf16[4,32,128]{2,1,0:T(8,128)(2,1)} %refs_3_.2), channel_id=1, source_target_pairs={{0,4},{4,0},{8,12},{12,8},{1,5},{5,1},{9,13},{13,9},{2,6},{6,2},{1... | collective-permute-start | bytes 98312 | tf_op jit(solution)/shard_map/ppermute | solution.py:96
  7.4 0.0 collective-permute-start.7
  7.4 0.0 copy-done.1
  7.4 0.0 copy-done
  7.4 0.0 copy-done.2
  7.5 1.5 %shard_map.91 = (f32[4,32,128]{2,1,0:T(8,128)S(1)}, f32[4,32,128]{2,1,0:T(8,128)S(1)}, bf16[2,4,128,128]{3,2,1,0:T(8,128)(2,1)S(1)}, f32[32,128]{1,0:T(8,128)S(1...) custom-call(s32[1,32]{1,0:T(1,128)S(1)} %bitcast.2, ...), custom_call_target="tpu_custom_call" | custom-call | flops 268435456 | tf_op jit(solution)/shard_map/pallas_call | solution.py:397
  9.0 0.4 %collective-permute-done.4.refs_2_ = bf16[4,32,128]{2,1,0:T(8,128)(2,1)S(1)} collective-permute-done((bf16[4,32,128]{2,1,0:T(8,128)(2,1)}, bf16[4,32,128]{2,1,0:T(8,128)(2,1)S(1)}, u32[]{:S(2)}, u32[]{:S(2)}) %collective-permute-start.4) | collective-permute-done | bytes 32800 | tf_op jit(solution)/shard_map/ppermute | solution.py:96
  9.3 0.2 %collective-permute-start.5 = (bf16[4,32,128]{2,1,0:T(8,128)(2,1)S(1)}, bf16[4,32,128]{2,1,0:T(8,128)(2,1)S(1)}, u32[]{:S(2)}, u32[]{:S(2)}) collective-permute-start(bf16[4,32,128]{2,1,0:T(8,128)(2,1)S(1)} %collective-permute-done.4.refs_2_), channel_id=1, source_target_pairs={{0,1},{1,0},{2,3},{3,2},{4,5},{5,4},{6,7},{7,6},{8,9},{9,8},{10,11... | collective-permute-start | bytes 98312 | tf_op jit(solution)/shard_map/ppermute | solution.py:96
  9.5 2.1 %collective-permute-done.2.refs_1_ = bf16[4,32,128]{2,1,0:T(8,128)(2,1)S(1)} collective-permute-done((bf16[4,32,128]{2,1,0:T(8,128)(2,1)}, bf16[4,32,128]{2,1,0:T(8,128)(2,1)S(1)}, u32[]{:S(2)}, u32[]{:S(2)}) %collective-permute-start.2) | collective-permute-done | bytes 32800 | tf_op jit(solution)/shard_map/ppermute | solution.py:96
  11.7 0.0 collective-permute-start.3
  11.7 0.0 collective-permute-done.refs_0_
  11.7 0.5 %collective-permute-start.1 = (bf16[4,32,128]{2,1,0:T(8,128)(2,1)S(1)}, bf16[4,32,128]{2,1,0:T(8,128)(2,1)S(1)}, u32[]{:S(2)}, u32[]{:S(2)}) collective-permute-start(bf16[4,32,128]{2,1,0:T(8,128)(2,1)S(1)} %collective-permute-done.refs_0_), channel_id=1, source_target_pairs={{0,1},{1,0},{2,3},{3,2},{4,5},{5,4},{6,7},{7,6},{8,9},{9,8},{10,11... | collective-permute-start | bytes 98312 | tf_op jit(solution)/shard_map/ppermute | solution.py:96
  12.2 0.0 collective-permute-done.7.refs_3_
  12.2 0.4 %shard_map.92 = (f32[16,32,128]{2,1,0:T(8,128)S(1)}, f32[16,32,128]{2,1,0:T(8,128)S(1)}, bf16[5,128,128]{2,1,0:T(8,128)(2,1)S(1)}) custom-call(bf16[4,32,128]{2,1,0:T(8,128)(2,1)S(1)} %collective-permute-done.refs_0_, bf16[4,32,128]{2,1,0:T(8,128)(2,1)S(1)} %collective-permute-done.2.refs_1_, bf16[4,32,128]{2,1,0:T(8,128)(2,1)S(1)} %collective-permute-done.4.refs_2_, ...), custom_call_target="tpu_custom_call" | custom-call | flops 268435456 | tf_op jit(solution)/shard_map/pallas_call | solution.py:397
  12.6 0.0 collective-permute-done.6.refs_0_
  12.6 0.6 %shard_map.93 = (f32[20,32,128]{2,1,0:T(8,128)S(1)}, f32[2,32,8,128]{3,2,1,0:T(8,128)S(1)}, f32[18,8,128]{2,1,0:T(8,128)S(1)}, bf16[2,4,128,128]{3,2,1,0:T(8,128)(2,1)S(1)}) custom-call(bf16[2,4,64,128]{3,2,1,0:T(8,128)(2,1)S(1)} %collective-permute-done.6.refs_0_, ...), custom_call_target="tpu_custom_call", output_to_operand_aliasing={{3}: (4, {})} | custom-call | flops 268435456 | tf_op jit(solution)/shard_map/pallas_call | solution.py:397
  13.2 0.0 collective-permute-done.5.refs_2_
  13.2 0.0 collective-permute-done.3.refs_1_
  13.2 0.0 collective-permute-done.1.refs_0_
  13.2 2.5 %shard_map.94 = bf16[4,16,128]{2,1,0:T(8,128)(2,1)} custom-call(bf16[4,32,128]{2,1,0:T(8,128)(2,1)S(1)} %collective-permute-done.1.refs_0_, bf16[4,32,128]{2,1,0:T(8,128)(2,1)S(1)} %collective-permute-done.3.refs_1_, bf16[4,32,128]{2,1,0:T(8,128)(2,1)S(1)} %collective-permute-done.5.refs_2_, f32[2,128]{1,0:T(2,128)S(1)} %copy-done, f32[2,128]{1,0:T(2,128)S(1)} %copy-done.1, ...), custom_call_target="tpu_custom_call" | custom-call | flops 262144 | tf_op jit(solution)/shard_map/pallas_call | solution.py:397
Async XLA Ops:
  0.0 7.4 %copy-start.1 = (f32[2,128]{1,0:T(2,128)S(1)}, f32[2,128]{1,0:T(2,128)}, u32[]{:S(2)}) copy-start(f32[2,128]{1,0:T(2,128)} %refs_4_.3) | copy-start | bytes 3076
  0.0 7.4 %copy-start = (f32[2,128]{1,0:T(2,128)S(1)}, f32[2,128]{1,0:T(2,128)}, u32[]{:S(2)}) copy-start(f32[2,128]{1,0:T(2,128)} %refs_3_.3) | copy-start | bytes 3076
  0.0 7.4 %copy-start.2 = (s32[32]{0:T(128)S(1)}, s32[32]{0:T(128)}, u32[]{:S(2)}) copy-start(s32[32]{0:T(128)} %param.10) | copy-start | bytes 388
  0.0 12.6 %collective-permute-start.6 = (bf16[2,4,64,128]{3,2,1,0:T(8,128)(2,1)}, bf16[2,4,64,128]{3,2,1,0:T(8,128)(2,1)S(1)}, u32[]{:S(2)}, u32[]{:S(2)}) collective-permute-start(bf16[2,4,64,128]{3,2,1,0:T(8,128)(2,1)} %bitcast.3), channel_id=1, source_target_pairs={{0,2},{2,0},{1,3},{3,1},{4,6},{6,4},{5,7},{7,5},{8,10},{10,8},{9,1... | collective-permute-start | bytes 393224 | tf_op jit(solution)/shard_map/ppermute | solution.py:96
  3.0 6.3 %collective-permute-start.4 = (bf16[4,32,128]{2,1,0:T(8,128)(2,1)}, bf16[4,32,128]{2,1,0:T(8,128)(2,1)S(1)}, u32[]{:S(2)}, u32[]{:S(2)}) collective-permute-start(bf16[4,32,128]{2,1,0:T(8,128)(2,1)} %refs_3_.2), channel_id=1, source_target_pairs={{0,12},{4,8},{8,4},{12,0},{1,13},{5,9},{9,5},{13,1},{2,14},{6,10},... | collective-permute-start | bytes 98312 | tf_op jit(solution)/shard_map/ppermute | solution.py:96
  6.6 5.0 %collective-permute-start.2 = (bf16[4,32,128]{2,1,0:T(8,128)(2,1)}, bf16[4,32,128]{2,1,0:T(8,128)(2,1)S(1)}, u32[]{:S(2)}, u32[]{:S(2)}) collective-permute-start(bf16[4,32,128]{2,1,0:T(8,128)(2,1)} %refs_3_.2), channel_id=1, source_target_pairs={{0,8},{4,12},{8,0},{12,4},{1,9},{5,13},{9,1},{13,5},{2,10},{6,14},... | collective-permute-start | bytes 98312 | tf_op jit(solution)/shard_map/ppermute | solution.py:96
  6.6 5.0 %collective-permute-start = (bf16[4,32,128]{2,1,0:T(8,128)(2,1)}, bf16[4,32,128]{2,1,0:T(8,128)(2,1)S(1)}, u32[]{:S(2)}, u32[]{:S(2)}) collective-permute-start(bf16[4,32,128]{2,1,0:T(8,128)(2,1)} %refs_3_.2), channel_id=1, source_target_pairs={{0,4},{4,0},{8,12},{12,8},{1,5},{5,1},{9,13},{13,9},{2,6},{6,2},{1... | collective-permute-start | bytes 98312 | tf_op jit(solution)/shard_map/ppermute | solution.py:96
  7.4 4.8 %collective-permute-start.7 = (bf16[4,32,128]{2,1,0:T(8,128)(2,1)}, bf16[4,32,128]{2,1,0:T(8,128)(2,1)S(1)}, u32[]{:S(2)}, u32[]{:S(2)}) collective-permute-start(bf16[4,32,128]{2,1,0:T(8,128)(2,1)} %refs_3_.2), channel_id=1, source_target_pairs={{0,1},{1,0},{2,3},{3,2},{4,5},{5,4},{6,7},{7,6},{8,9},{9,8},{10,11... | collective-permute-start | bytes 98312 | tf_op jit(solution)/shard_map/ppermute | solution.py:96
  9.3 3.9 %collective-permute-start.5 = (bf16[4,32,128]{2,1,0:T(8,128)(2,1)S(1)}, bf16[4,32,128]{2,1,0:T(8,128)(2,1)S(1)}, u32[]{:S(2)}, u32[]{:S(2)}) collective-permute-start(bf16[4,32,128]{2,1,0:T(8,128)(2,1)S(1)} %collective-permute-done.4.refs_2_), channel_id=1, source_target_pairs={{0,1},{1,0},{2,3},{3,2},{4,5},{5,4},{6,7},{7,6},{8,9},{9,8},{10,11... | collective-permute-start | bytes 98312 | tf_op jit(solution)/shard_map/ppermute | solution.py:96
  11.7 1.5 %collective-permute-start.3 = (bf16[4,32,128]{2,1,0:T(8,128)(2,1)S(1)}, bf16[4,32,128]{2,1,0:T(8,128)(2,1)S(1)}, u32[]{:S(2)}, u32[]{:S(2)}) collective-permute-start(bf16[4,32,128]{2,1,0:T(8,128)(2,1)S(1)} %collective-permute-done.2.refs_1_), channel_id=1, source_target_pairs={{0,1},{1,0},{2,3},{3,2},{4,5},{5,4},{6,7},{7,6},{8,9},{9,8},{10,11... | collective-permute-start | bytes 98312 | tf_op jit(solution)/shard_map/ppermute | solution.py:96
  11.7 1.5 %collective-permute-start.1 = (bf16[4,32,128]{2,1,0:T(8,128)(2,1)S(1)}, bf16[4,32,128]{2,1,0:T(8,128)(2,1)S(1)}, u32[]{:S(2)}, u32[]{:S(2)}) collective-permute-start(bf16[4,32,128]{2,1,0:T(8,128)(2,1)S(1)} %collective-permute-done.refs_0_), channel_id=1, source_target_pairs={{0,1},{1,0},{2,3},{3,2},{4,5},{5,4},{6,7},{7,6},{8,9},{9,8},{10,11... | collective-permute-start | bytes 98312 | tf_op jit(solution)/shard_map/ppermute | solution.py:96

commit v5 on v4

--- a/solution.py
+++ b/solution.py
@@ -158,7 +158,7 @@
     def enter(self, blocks, gain_ref, bias_ref, gw_ref, gate_ref, x_ref):
         x = jnp.concatenate([b.reshape(self.area, self.c) for b in blocks], 0)
         normed = self.norm(x, gain_ref, bias_ref, 0)
-        gate_ref[...] = jnp.tanh(mm(normed, gw_ref[0])).reshape(gate_ref.shape)
+        gate_ref[...] = (1.0 + jnp.tanh(mm(normed, gw_ref[0]))).reshape(gate_ref.shape)
         x_ref[...] = x.astype(jnp.float32).reshape(x_ref.shape)
         return normed
 
@@ -320,7 +320,7 @@
         centred = both[:, :h]
         spread = jnp.mean(centred * centred, axis=1, keepdims=True)
         update = both[:, h:] * lax.rsqrt(spread + epsilon) + shift_ref[layer, 0:1]
-        return (residual + (update * half_gate + update)).astype(jnp.bfloat16)
+        return (residual + update * half_gate).astype(jnp.bfloat16)
 
     half_gate = place.columns((gate0_ref, gate1_ref, gate2_ref))
     residual = place.columns((x0_ref, x1_ref, x2_ref))
@@ -341,7 +341,7 @@
         columns = place.column_masks(mask_ref, (t,))[None]
         shape = (length, chip, h)
         r1_ref[t - 1] = gated(p[at, :h].reshape(shape), p[at, h:].reshape(shape) * columns)
-    half_gate = jnp.tanh(mm(mine_normed, gw_ref[1]))
+    half_gate = 1.0 + jnp.tanh(mm(mine_normed, gw_ref[1]))
 
     acc = [jnp.zeros((chip, h), jnp.float32) for _ in range(2 * size)]
     for k in range(length):

time: 15.8 us -> 15.8 us (level)
  no operation moved by 1% of the time
where the time goes in v5:
time: 15.8 us; the launch traced here: 15.7 us
  starting transfers between devices  8.15 us (52%)
  Pallas kernels  4.95 us (31%)
  waiting for transfers between devices  2.52 us (16%)
    ppermute x8, starting transfers between devices, swap(): return lax.ppermute(value, axis, [(i, i ^ step) for i in range(count)])  8.15 us
    pallas_call x4, Pallas kernels, call(): pl.pallas_call(kernel, out_shape=out_shape, in_specs=[VMEM] * len(near) +...  4.95 us
    ppermute x8, waiting for transfers between devices, swap(): return lax.ppermute(value, axis, [(i, i ^ step) for i in range(count)])  2.52 us
  transfers between devices with their start and end apart: 8, of which 2 were waited for; matrix products, arithmetic and copies ran while one was open for 0% of the time, Pallas kernels for 16%

profile of v5, /device:TPU:0, one launch (start us, length us, event | category | flops | bytes accessed | tf_op | source)
XLA Modules:
  0.0 15.7 jit_solution(3617781887008694481)
XLA Ops:
  0.0 0.0 copy-start.1
  0.0 0.0 copy-start
  0.0 0.0 copy-start.2
  0.0 3.0 %collective-permute-start.6 = (bf16[2,4,64,128]{3,2,1,0:T(8,128)(2,1)}, bf16[2,4,64,128]{3,2,1,0:T(8,128)(2,1)S(1)}, u32[]{:S(2)}, u32[]{:S(2)}) collective-permute-start(bf16[2,4,64,128]{3,2,1,0:T(8,128)(2,1)} %bitcast.3), channel_id=1, source_target_pairs={{0,2},{2,0},{1,3},{3,1},{4,6},{6,4},{5,7},{7,5},{8,10},{10,8},{9,1... | collective-permute-start | bytes 393224 | tf_op jit(solution)/shard_map/ppermute | solution.py:96
  3.0 3.6 %collective-permute-start.4 = (bf16[4,32,128]{2,1,0:T(8,128)(2,1)}, bf16[4,32,128]{2,1,0:T(8,128)(2,1)S(1)}, u32[]{:S(2)}, u32[]{:S(2)}) collective-permute-start(bf16[4,32,128]{2,1,0:T(8,128)(2,1)} %refs_3_.2), channel_id=1, source_target_pairs={{0,12},{4,8},{8,4},{12,0},{1,13},{5,9},{9,5},{13,1},{2,14},{6,10},... | collective-permute-start | bytes 98312 | tf_op jit(solution)/shard_map/ppermute | solution.py:96
  6.6 0.0 collective-permute-start.2
  6.6 0.8 %collective-permute-start = (bf16[4,32,128]{2,1,0:T(8,128)(2,1)}, bf16[4,32,128]{2,1,0:T(8,128)(2,1)S(1)}, u32[]{:S(2)}, u32[]{:S(2)}) collective-permute-start(bf16[4,32,128]{2,1,0:T(8,128)(2,1)} %refs_3_.2), channel_id=1, source_target_pairs={{0,4},{4,0},{8,12},{12,8},{1,5},{5,1},{9,13},{13,9},{2,6},{6,2},{1... | collective-permute-start | bytes 98312 | tf_op jit(solution)/shard_map/ppermute | solution.py:96
  7.4 0.0 collective-permute-start.7
  7.4 0.0 copy-done.1
  7.4 0.0 copy-done
  7.4 0.0 copy-done.2
  7.5 1.5 %shard_map.91 = (f32[4,32,128]{2,1,0:T(8,128)S(1)}, f32[4,32,128]{2,1,0:T(8,128)S(1)}, bf16[2,4,128,128]{3,2,1,0:T(8,128)(2,1)S(1)}, f32[32,128]{1,0:T(8,128)S(1...) custom-call(s32[1,32]{1,0:T(1,128)S(1)} %bitcast.2, ...), custom_call_target="tpu_custom_call" | custom-call | flops 268435456 | tf_op jit(solution)/shard_map/pallas_call | solution.py:397
  9.0 0.4 %collective-permute-done.4.refs_2_ = bf16[4,32,128]{2,1,0:T(8,128)(2,1)S(1)} collective-permute-done((bf16[4,32,128]{2,1,0:T(8,128)(2,1)}, bf16[4,32,128]{2,1,0:T(8,128)(2,1)S(1)}, u32[]{:S(2)}, u32[]{:S(2)}) %collective-permute-start.4) | collective-permute-done | bytes 32800 | tf_op jit(solution)/shard_map/ppermute | solution.py:96
  9.3 0.2 %collective-permute-start.5 = (bf16[4,32,128]{2,1,0:T(8,128)(2,1)S(1)}, bf16[4,32,128]{2,1,0:T(8,128)(2,1)S(1)}, u32[]{:S(2)}, u32[]{:S(2)}) collective-permute-start(bf16[4,32,128]{2,1,0:T(8,128)(2,1)S(1)} %collective-permute-done.4.refs_2_), channel_id=1, source_target_pairs={{0,1},{1,0},{2,3},{3,2},{4,5},{5,4},{6,7},{7,6},{8,9},{9,8},{10,11... | collective-permute-start | bytes 98312 | tf_op jit(solution)/shard_map/ppermute | solution.py:96
  9.5 2.1 %collective-permute-done.2.refs_1_ = bf16[4,32,128]{2,1,0:T(8,128)(2,1)S(1)} collective-permute-done((bf16[4,32,128]{2,1,0:T(8,128)(2,1)}, bf16[4,32,128]{2,1,0:T(8,128)(2,1)S(1)}, u32[]{:S(2)}, u32[]{:S(2)}) %collective-permute-start.2) | collective-permute-done | bytes 32800 | tf_op jit(solution)/shard_map/ppermute | solution.py:96
  11.7 0.0 collective-permute-start.3
  11.7 0.0 collective-permute-done.refs_0_
  11.7 0.5 %collective-permute-start.1 = (bf16[4,32,128]{2,1,0:T(8,128)(2,1)S(1)}, bf16[4,32,128]{2,1,0:T(8,128)(2,1)S(1)}, u32[]{:S(2)}, u32[]{:S(2)}) collective-permute-start(bf16[4,32,128]{2,1,0:T(8,128)(2,1)S(1)} %collective-permute-done.refs_0_), channel_id=1, source_target_pairs={{0,1},{1,0},{2,3},{3,2},{4,5},{5,4},{6,7},{7,6},{8,9},{9,8},{10,11... | collective-permute-start | bytes 98312 | tf_op jit(solution)/shard_map/ppermute | solution.py:96
  12.2 0.0 collective-permute-done.7.refs_3_
  12.2 0.4 %shard_map.92 = (f32[16,32,128]{2,1,0:T(8,128)S(1)}, f32[16,32,128]{2,1,0:T(8,128)S(1)}, bf16[5,128,128]{2,1,0:T(8,128)(2,1)S(1)}) custom-call(bf16[4,32,128]{2,1,0:T(8,128)(2,1)S(1)} %collective-permute-done.refs_0_, bf16[4,32,128]{2,1,0:T(8,128)(2,1)S(1)} %collective-permute-done.2.refs_1_, bf16[4,32,128]{2,1,0:T(8,128)(2,1)S(1)} %collective-permute-done.4.refs_2_, ...), custom_call_target="tpu_custom_call" | custom-call | flops 268435456 | tf_op jit(solution)/shard_map/pallas_call | solution.py:397
  12.6 0.0 collective-permute-done.6.refs_0_
  12.6 0.6 %shard_map.93 = (f32[20,32,128]{2,1,0:T(8,128)S(1)}, f32[2,32,8,128]{3,2,1,0:T(8,128)S(1)}, f32[18,8,128]{2,1,0:T(8,128)S(1)}, bf16[2,4,128,128]{3,2,1,0:T(8,128)(2,1)S(1)}) custom-call(bf16[2,4,64,128]{3,2,1,0:T(8,128)(2,1)S(1)} %collective-permute-done.6.refs_0_, ...), custom_call_target="tpu_custom_call", output_to_operand_aliasing={{3}: (4, {})} | custom-call | flops 268435456 | tf_op jit(solution)/shard_map/pallas_call | solution.py:397
  13.2 0.0 collective-permute-done.5.refs_2_
  13.2 0.0 collective-permute-done.3.refs_1_
  13.2 0.0 collective-permute-done.1.refs_0_
  13.2 2.5 %shard_map.94 = bf16[4,16,128]{2,1,0:T(8,128)(2,1)} custom-call(bf16[4,32,128]{2,1,0:T(8,128)(2,1)S(1)} %collective-permute-done.1.refs_0_, bf16[4,32,128]{2,1,0:T(8,128)(2,1)S(1)} %collective-permute-done.3.refs_1_, bf16[4,32,128]{2,1,0:T(8,128)(2,1)S(1)} %collective-permute-done.5.refs_2_, f32[2,128]{1,0:T(2,128)S(1)} %copy-done, f32[2,128]{1,0:T(2,128)S(1)} %copy-done.1, ...), custom_call_target="tpu_custom_call" | custom-call | flops 262144 | tf_op jit(solution)/shard_map/pallas_call | solution.py:397
Async XLA Ops:
  0.0 7.4 %copy-start.1 = (f32[2,128]{1,0:T(2,128)S(1)}, f32[2,128]{1,0:T(2,128)}, u32[]{:S(2)}) copy-start(f32[2,128]{1,0:T(2,128)} %refs_4_.3) | copy-start | bytes 3076
  0.0 7.4 %copy-start = (f32[2,128]{1,0:T(2,128)S(1)}, f32[2,128]{1,0:T(2,128)}, u32[]{:S(2)}) copy-start(f32[2,128]{1,0:T(2,128)} %refs_3_.3) | copy-start | bytes 3076
  0.0 7.4 %copy-start.2 = (s32[32]{0:T(128)S(1)}, s32[32]{0:T(128)}, u32[]{:S(2)}) copy-start(s32[32]{0:T(128)} %param.10) | copy-start | bytes 388
  0.0 12.6 %collective-permute-start.6 = (bf16[2,4,64,128]{3,2,1,0:T(8,128)(2,1)}, bf16[2,4,64,128]{3,2,1,0:T(8,128)(2,1)S(1)}, u32[]{:S(2)}, u32[]{:S(2)}) collective-permute-start(bf16[2,4,64,128]{3,2,1,0:T(8,128)(2,1)} %bitcast.3), channel_id=1, source_target_pairs={{0,2},{2,0},{1,3},{3,1},{4,6},{6,4},{5,7},{7,5},{8,10},{10,8},{9,1... | collective-permute-start | bytes 393224 | tf_op jit(solution)/shard_map/ppermute | solution.py:96
  3.0 6.3 %collective-permute-start.4 = (bf16[4,32,128]{2,1,0:T(8,128)(2,1)}, bf16[4,32,128]{2,1,0:T(8,128)(2,1)S(1)}, u32[]{:S(2)}, u32[]{:S(2)}) collective-permute-start(bf16[4,32,128]{2,1,0:T(8,128)(2,1)} %refs_3_.2), channel_id=1, source_target_pairs={{0,12},{4,8},{8,4},{12,0},{1,13},{5,9},{9,5},{13,1},{2,14},{6,10},... | collective-permute-start | bytes 98312 | tf_op jit(solution)/shard_map/ppermute | solution.py:96
  6.6 5.0 %collective-permute-start.2 = (bf16[4,32,128]{2,1,0:T(8,128)(2,1)}, bf16[4,32,128]{2,1,0:T(8,128)(2,1)S(1)}, u32[]{:S(2)}, u32[]{:S(2)}) collective-permute-start(bf16[4,32,128]{2,1,0:T(8,128)(2,1)} %refs_3_.2), channel_id=1, source_target_pairs={{0,8},{4,12},{8,0},{12,4},{1,9},{5,13},{9,1},{13,5},{2,10},{6,14},... | collective-permute-start | bytes 98312 | tf_op jit(solution)/shard_map/ppermute | solution.py:96
  6.6 5.0 %collective-permute-start = (bf16[4,32,128]{2,1,0:T(8,128)(2,1)}, bf16[4,32,128]{2,1,0:T(8,128)(2,1)S(1)}, u32[]{:S(2)}, u32[]{:S(2)}) collective-permute-start(bf16[4,32,128]{2,1,0:T(8,128)(2,1)} %refs_3_.2), channel_id=1, source_target_pairs={{0,4},{4,0},{8,12},{12,8},{1,5},{5,1},{9,13},{13,9},{2,6},{6,2},{1... | collective-permute-start | bytes 98312 | tf_op jit(solution)/shard_map/ppermute | solution.py:96
  7.4 4.8 %collective-permute-start.7 = (bf16[4,32,128]{2,1,0:T(8,128)(2,1)}, bf16[4,32,128]{2,1,0:T(8,128)(2,1)S(1)}, u32[]{:S(2)}, u32[]{:S(2)}) collective-permute-start(bf16[4,32,128]{2,1,0:T(8,128)(2,1)} %refs_3_.2), channel_id=1, source_target_pairs={{0,1},{1,0},{2,3},{3,2},{4,5},{5,4},{6,7},{7,6},{8,9},{9,8},{10,11... | collective-permute-start | bytes 98312 | tf_op jit(solution)/shard_map/ppermute | solution.py:96
  9.3 3.9 %collective-permute-start.5 = (bf16[4,32,128]{2,1,0:T(8,128)(2,1)S(1)}, bf16[4,32,128]{2,1,0:T(8,128)(2,1)S(1)}, u32[]{:S(2)}, u32[]{:S(2)}) collective-permute-start(bf16[4,32,128]{2,1,0:T(8,128)(2,1)S(1)} %collective-permute-done.4.refs_2_), channel_id=1, source_target_pairs={{0,1},{1,0},{2,3},{3,2},{4,5},{5,4},{6,7},{7,6},{8,9},{9,8},{10,11... | collective-permute-start | bytes 98312 | tf_op jit(solution)/shard_map/ppermute | solution.py:96
  11.7 1.5 %collective-permute-start.3 = (bf16[4,32,128]{2,1,0:T(8,128)(2,1)S(1)}, bf16[4,32,128]{2,1,0:T(8,128)(2,1)S(1)}, u32[]{:S(2)}, u32[]{:S(2)}) collective-permute-start(bf16[4,32,128]{2,1,0:T(8,128)(2,1)S(1)} %collective-permute-done.2.refs_1_), channel_id=1, source_target_pairs={{0,1},{1,0},{2,3},{3,2},{4,5},{5,4},{6,7},{7,6},{8,9},{9,8},{10,11... | collective-permute-start | bytes 98312 | tf_op jit(solution)/shard_map/ppermute | solution.py:96
  11.7 1.5 %collective-permute-start.1 = (bf16[4,32,128]{2,1,0:T(8,128)(2,1)S(1)}, bf16[4,32,128]{2,1,0:T(8,128)(2,1)S(1)}, u32[]{:S(2)}, u32[]{:S(2)}) collective-permute-start(bf16[4,32,128]{2,1,0:T(8,128)(2,1)S(1)} %collective-permute-done.refs_0_), channel_id=1, source_target_pairs={{0,1},{1,0},{2,3},{3,2},{4,5},{5,4},{6,7},{7,6},{8,9},{9,8},{10,11... | collective-permute-start | bytes 98312 | tf_op jit(solution)/shard_map/ppermute | solution.py:96
